TPU v7x, 8 devices: a whole 2x2x1 slice. The times are simulated.
8 devices in a mesh: dp: 2 (over z, y), sp: 4 (over x, core).
Axes of the slice: x: 2, y: 2, z: 1, core: 2. Of those that a mesh axis runs over, the one named last changes fastest.
Arguments:
- x: bfloat16 [2, 4096, 4096], P('dp', 'sp'), parts along dimension 0
- segment_ids: int32 [2, 4096], P('dp', 'sp'), parts along dimension 0
- positions: int32 [2, 4096], P('dp', 'sp'), parts along dimension 0
- out_grad: bfloat16 [2, 4096, 4096], P('dp', 'sp'), parts along dimension 0
- norm_scale: bfloat16 [4096], replicated
- w_q: bfloat16 [4096, 4096], replicated
- w_k: bfloat16 [4096, 256], replicated
- w_v: bfloat16 [4096, 256], replicated
- w_o: bfloat16 [4096, 4096], replicated
- b_o: bfloat16 [4096], replicated
Outputs:
- output 1: bfloat16 [2, 4096, 4096], P('dp', 'sp'), parts along dimension 0
- output 2: bfloat16 [2, 4096, 4096], P('dp', 'sp'), parts along dimension 0
- output 3: bfloat16 [8192], P('dp'), parts along dimension 0
- output 4: bfloat16 [8192, 4096], P('dp'), parts along dimension 0
- output 5: bfloat16 [8192, 256], P('dp'), parts along dimension 0
- output 6: bfloat16 [8192, 256], P('dp'), parts along dimension 0
- output 7: bfloat16 [8192, 4096], P('dp'), parts along dimension 0
- output 8: bfloat16 [8192], P('dp'), parts along dimension 0
There are 2 independent parts. A program takes and returns all parts, laid end to end along the dimension named above; an argument that names none is the same for every part.
All inputs are finite; a program needn't handle non-finite values.
Results may differ from a plain program's by a relative error of at most 0.017504.
Values are sent between devices in bfloat16 or wider.
A program may use at most 1 GiB of HBM per device.

v0:
```python
import jax
import jax.numpy as jnp
from jax import lax
from jax.sharding import PartitionSpec as P

WINDOW = 2048
QUERY_BLOCK = 128
NORM_EPS = 1e-6
ROPE_BASE = 10000.0
NEG_BIG = -1e30


def rms_norm(x_f32, gain_f32):
    mean_sq = jnp.mean(x_f32 * x_f32, axis=-1, keepdims=True)
    return (x_f32 * lax.rsqrt(mean_sq + NORM_EPS) * (1.0 + gain_f32)).astype(jnp.bfloat16)


def rotary(head_vals, positions, rot_sign):
    rot_dim = head_vals.shape[-1] // 2
    half_dim = rot_dim // 2
    inv_freq = ROPE_BASE ** (-(jnp.arange(half_dim, dtype=jnp.float32) * 2.0 / rot_dim))
    angles = positions.astype(jnp.float32)[:, :, None, None] * inv_freq
    cos_a = jnp.cos(angles)
    sin_a = rot_sign * jnp.sin(angles)
    first_half = head_vals[..., :half_dim]
    second_half = head_vals[..., half_dim:rot_dim]
    return jnp.concatenate([first_half * cos_a - second_half * sin_a, second_half * cos_a + first_half * sin_a, head_vals[..., rot_dim:]], axis=-1)


def block_probs(q_blk, k_blk, q_seg, k_seg, key_first):
    offsets = jnp.arange(WINDOW + QUERY_BLOCK)
    row_idx = jnp.arange(QUERY_BLOCK)[:, None]
    in_band = (offsets[None, :] > row_idx) & (offsets[None, :] <= row_idx + WINDOW) & (key_first + offsets >= 0)[None, :]
    allowed = (q_seg[:, :, None] == k_seg[:, None, :]) & in_band[None]
    scores = jnp.einsum("bqhe,bke->bhqk", q_blk, k_blk, preferred_element_type=jnp.float32)
    scores = jnp.where(allowed[:, None], scores, NEG_BIG)
    exp_scores = jnp.exp(scores - jnp.max(scores, axis=-1, keepdims=True))
    return exp_scores / jnp.sum(exp_scores, axis=-1, keepdims=True)


def band_forward(queries, keys_pad, values_pad, q_seg, k_seg_pad, key_first):
    key_span = WINDOW + QUERY_BLOCK

    def block_step(block_idx, out_acc):
        q_start = block_idx * QUERY_BLOCK
        k_blk = lax.dynamic_slice_in_dim(keys_pad, q_start, key_span, axis=1)
        v_blk = lax.dynamic_slice_in_dim(values_pad, q_start, key_span, axis=1)
        attn_prob = block_probs(lax.dynamic_slice_in_dim(queries, q_start, QUERY_BLOCK, axis=1), k_blk, lax.dynamic_slice_in_dim(q_seg, q_start, QUERY_BLOCK, axis=1), lax.dynamic_slice_in_dim(k_seg_pad, q_start, key_span, axis=1), key_first + q_start)
        o_blk = jnp.einsum("bhqk,bke->bqhe", attn_prob.astype(jnp.bfloat16), v_blk, preferred_element_type=jnp.float32)
        return lax.dynamic_update_slice_in_dim(out_acc, o_blk.astype(jnp.bfloat16), q_start, axis=1)

    return lax.fori_loop(0, queries.shape[1] // QUERY_BLOCK, block_step, jnp.zeros_like(queries))


def band_backward(queries, keys_pad, values_pad, q_seg, k_seg_pad, key_first, d_out):
    key_span = WINDOW + QUERY_BLOCK

    def block_step(block_idx, loop_state):
        dq_acc, dk_acc, dv_acc = loop_state
        q_start = block_idx * QUERY_BLOCK
        q_blk = lax.dynamic_slice_in_dim(queries, q_start, QUERY_BLOCK, axis=1)
        do_blk = lax.dynamic_slice_in_dim(d_out, q_start, QUERY_BLOCK, axis=1)
        k_blk = lax.dynamic_slice_in_dim(keys_pad, q_start, key_span, axis=1)
        v_blk = lax.dynamic_slice_in_dim(values_pad, q_start, key_span, axis=1)
        attn_prob = block_probs(q_blk, k_blk, lax.dynamic_slice_in_dim(q_seg, q_start, QUERY_BLOCK, axis=1), lax.dynamic_slice_in_dim(k_seg_pad, q_start, key_span, axis=1), key_first + q_start)
        d_prob = jnp.einsum("bqhe,bke->bhqk", do_blk, v_blk, preferred_element_type=jnp.float32)
        d_score = (attn_prob * (d_prob - jnp.sum(d_prob * attn_prob, axis=-1, keepdims=True))).astype(jnp.bfloat16)
        dq_blk = jnp.einsum("bhqk,bke->bqhe", d_score, k_blk, preferred_element_type=jnp.float32).astype(jnp.bfloat16)
        dk_blk = jnp.einsum("bhqk,bqhe->bke", d_score, q_blk, preferred_element_type=jnp.float32)
        dv_blk = jnp.einsum("bhqk,bqhe->bke", attn_prob.astype(jnp.bfloat16), do_blk, preferred_element_type=jnp.float32)
        dq_acc = lax.dynamic_update_slice_in_dim(dq_acc, dq_blk, q_start, axis=1)
        dk_acc = lax.dynamic_update_slice_in_dim(dk_acc, lax.dynamic_slice_in_dim(dk_acc, q_start, key_span, axis=1) + dk_blk, q_start, axis=1)
        dv_acc = lax.dynamic_update_slice_in_dim(dv_acc, lax.dynamic_slice_in_dim(dv_acc, q_start, key_span, axis=1) + dv_blk, q_start, axis=1)
        return dq_acc, dk_acc, dv_acc

    init_state = (jnp.zeros_like(queries), jnp.zeros(keys_pad.shape, jnp.float32), jnp.zeros(values_pad.shape, jnp.float32))
    return lax.fori_loop(0, queries.shape[1] // QUERY_BLOCK, block_step, init_state)


def project_tokens(x, positions, norm_scale, w_q, w_k, w_v):
    batch_rows, chunk_len = x.shape[0], x.shape[1]
    head_dim = w_k.shape[1]
    x_f32 = x.astype(jnp.float32)
    normed, norm_pull = jax.vjp(rms_norm, x_f32, norm_scale.astype(jnp.float32))
    q_lin = jnp.dot(normed, w_q, preferred_element_type=jnp.float32).reshape(batch_rows, chunk_len, -1, head_dim)
    queries = (rotary(q_lin, positions, 1.0) * head_dim ** -0.5).astype(jnp.bfloat16)
    keys_loc = rotary(jnp.dot(normed, w_k, preferred_element_type=jnp.float32)[:, :, None, :], positions, 1.0)[:, :, 0, :].astype(jnp.bfloat16)
    values_loc = jnp.dot(normed, w_v, preferred_element_type=jnp.float32).astype(jnp.bfloat16)
    return x_f32, normed, norm_pull, queries, keys_loc, values_loc


def token_backward(norm_pull, normed, positions, out_grad, dq_tok, dk_loc, dv_loc, w_q, w_k, w_v):
    batch_rows, chunk_len = out_grad.shape[0], out_grad.shape[1]
    head_dim = w_k.shape[1]
    dq_lin = (rotary(dq_tok.astype(jnp.float32), positions, -1.0) * head_dim ** -0.5).astype(jnp.bfloat16).reshape(batch_rows, chunk_len, -1)
    dk_lin = rotary(dk_loc.astype(jnp.bfloat16).astype(jnp.float32)[:, :, None, :], positions, -1.0)[:, :, 0, :].astype(jnp.bfloat16)
    dv_lin = dv_loc.astype(jnp.bfloat16)
    d_normed = (jnp.einsum("bcn,dn->bcd", dq_lin, w_q, preferred_element_type=jnp.float32)
                + jnp.einsum("bce,de->bcd", dk_lin, w_k, preferred_element_type=jnp.float32)
                + jnp.einsum("bce,de->bcd", dv_lin, w_v, preferred_element_type=jnp.float32)).astype(jnp.bfloat16)
    w_q_part = jnp.einsum("bcd,bcn->dn", normed, dq_lin, preferred_element_type=jnp.float32)
    w_k_part = jnp.einsum("bcd,bce->de", normed, dk_lin, preferred_element_type=jnp.float32)
    w_v_part = jnp.einsum("bcd,bce->de", normed, dv_lin, preferred_element_type=jnp.float32)
    dx_norm, gain_part = norm_pull(d_normed)
    x_grad = (out_grad.astype(jnp.float32) + dx_norm).astype(jnp.bfloat16)
    return x_grad, gain_part, w_q_part, w_k_part, w_v_part


def solution(mesh):
    row_spec = P("dp", "sp", None)
    tok_spec = P("dp", "sp")
    mat_spec = P(None, None)
    grad_mat = P("dp", None)

    def local_step(x, seg_ids, positions, out_grad, norm_scale, w_q, w_k, w_v, w_o, b_o):
        batch_rows, chunk_len = x.shape[0], x.shape[1]
        x_f32, normed, norm_pull, queries, keys_loc, values_loc = project_tokens(x, positions, norm_scale, w_q, w_k, w_v)
        pad_keys = ((0, 0), (WINDOW, 0), (0, 0))
        q_heads = lax.all_to_all(queries, "sp", 2, 1, tiled=True)
        keys_pad = jnp.pad(lax.all_gather(keys_loc, "sp", axis=1, tiled=True), pad_keys)
        values_pad = jnp.pad(lax.all_gather(values_loc, "sp", axis=1, tiled=True), pad_keys)
        seg_all = lax.all_gather(seg_ids, "sp", axis=1, tiled=True)
        seg_pad = jnp.pad(seg_all, ((0, 0), (WINDOW, 0)))
        o_heads = band_forward(q_heads, keys_pad, values_pad, seg_all, seg_pad, -WINDOW)
        o_tok = lax.all_to_all(o_heads, "sp", 1, 2, tiled=True).reshape(batch_rows, chunk_len, -1)
        block_out = (x_f32 + jnp.dot(o_tok, w_o, preferred_element_type=jnp.float32) + b_o.astype(jnp.float32)).astype(jnp.bfloat16)
        d_o = jnp.einsum("bcd,nd->bcn", out_grad, w_o, preferred_element_type=jnp.float32).astype(jnp.bfloat16).reshape(queries.shape)
        w_o_part = jnp.einsum("bcn,bcd->nd", o_tok, out_grad, preferred_element_type=jnp.float32)
        b_o_part = jnp.sum(out_grad, axis=(0, 1), dtype=jnp.float32)
        do_heads = lax.all_to_all(d_o, "sp", 2, 1, tiled=True)
        dq_heads, dk_pad, dv_pad = band_backward(q_heads, keys_pad, values_pad, seg_all, seg_pad, -WINDOW, do_heads)
        dk_loc = lax.psum_scatter(dk_pad[:, WINDOW:], "sp", scatter_dimension=1, tiled=True)
        dv_loc = lax.psum_scatter(dv_pad[:, WINDOW:], "sp", scatter_dimension=1, tiled=True)
        dq_tok = lax.all_to_all(dq_heads, "sp", 1, 2, tiled=True)
        x_grad, gain_part, w_q_part, w_k_part, w_v_part = token_backward(norm_pull, normed, positions, out_grad, dq_tok, dk_loc, dv_loc, w_q, w_k, w_v)
        summed = lax.psum((gain_part, w_q_part, w_k_part, w_v_part, w_o_part, b_o_part), "sp")
        return (block_out, x_grad) + tuple(part_sum.astype(jnp.bfloat16) for part_sum in summed)

    return jax.shard_map(local_step, mesh=mesh,
                         in_specs=(row_spec, tok_spec, tok_spec, row_spec, P(None), mat_spec, mat_spec, mat_spec, mat_spec, P(None)),
                         out_specs=(row_spec, row_spec, P("dp"), grad_mat, grad_mat, grad_mat, grad_mat, P("dp")),
                         check_vma=False)
```

profile of v0, /device:TPU:0, one launch (start us, length us, event | category | flops | bytes accessed | tf_op | source)
XLA Modules:
  0.0 4321.4 jit_solution(17459345699487569591)
XLA Ops:
  19.7 55.6 %fusion.86 = bf16[1024,4096]{1,0:T(8,128)(2,1)} fusion(bf16[4096,4096]{1,0:T(8,128)(2,1)} %param.22, bf16[1,1024,4096]{2,1,0:T(8,128)(2,1)} %param.17), kind=kOutput, calls=%fused_computation.122 | convolution fusion | flops 34363932672 | bytes 50331648 | tf_op jit(solution)/shard_map/bcd,nd->bcn/dot_general | solution.py:127
  75.3 9.9 copy.90
  85.1 9.6 copy.64
  94.7 5.6 all-to-all-start.2
  100.4 44.1 %copy.74 = bf16[4096,4096]{1,0:T(8,128)(2,1)} copy(bf16[4096,4096]{0,1:T(8,128)(2,1)} %bitcast.250) | data formatting | bytes 67108864 | tf_op jit(solution)/shard_map/dot_general | solution.py:85
  144.5 43.5 %convolution_bitcast_fusion.5 = f32[1,1024,16,256]{1,3,2,0:T(8,128)} fusion(bf16[16,256,4096]{2,1,0:T(8,128)(2,1)} %bitcast.251, bf16[1,1024,4096]{2,1,0:T(8,128)(2,1)} %param.14, f32[4096]{0:T(1024)S(1)} %convert_add_fusion.2, f32[1024]{0:T(1024)S(1)} %fusion.126), kind=kOutput, calls=%fused_computation.105 | convolution fusion | flops 34376515584 | bytes 58740736 | tf_op jit(solution)/shard_map/dot_general | solution.py:85
  203.4 5.7 all-to-all-start
  209.2 6.6 fusion.92
  216.4 99.2 %all_gather.10 = s32[1,4096]{1,0:T(1,128)S(1)} all-gather(s32[1,1024]{1,0:T(1,128)S(1)} %copy-done.26), channel_id=1, replica_groups=mesh['dp'=2,'sp'=4] {'sp'}, dimensions={1}, use_global_device_ids=true | all-gather | bytes 20480 | tf_op jit(solution)/shard_map/all_gather | solution.py:122
  326.6 7.5 copy.65
  334.1 11.5 copy.58
  352.1 5.3 broadcast.452.clone2.1
  357.4 1010.5 %while.31 = (s32[]{:T(128)}, bf16[1,4096,4,256]{3,2,0,1:T(4,128)(2,1)}, f32[1,6144,256]{1,2,0:T(8,128)}, f32[1,6144,256]{2,1,0:T(8,128)}, bf16[1,6144,256]{2,1,0...) while((s32[]{:T(128)}, ...), condition=%wide.region_9.10_spmd, body=%wide.region_5.0_spmd.sunk | while | flops 2872871936 | bytes 106584696 | solution.py:77
  381.2 5.6 fusion.193
  412.8 5.6 fusion.193
  444.4 5.5 fusion.193
  476.0 5.5 fusion.193
  507.5 5.5 fusion.193
  539.1 5.5 fusion.193
  570.6 5.5 fusion.193
  602.1 5.5 fusion.193
  633.7 5.5 fusion.193
  665.2 5.5 fusion.193
  696.7 5.5 fusion.193
  728.2 5.5 fusion.193
  759.8 5.5 fusion.193
  791.3 5.5 fusion.193
  822.8 5.5 fusion.193
  854.4 5.5 fusion.193
  886.0 5.5 fusion.193
  917.5 5.6 fusion.193
  949.1 5.6 fusion.193
  980.7 5.6 fusion.193
  1012.4 5.6 fusion.193
  1044.0 5.6 fusion.193
  1075.7 5.6 fusion.193
  1107.3 5.6 fusion.193
  1139.0 5.6 fusion.193
  1170.6 5.6 fusion.193
  1202.2 5.6 fusion.193
  1233.8 5.6 fusion.193
  1265.4 5.6 fusion.193
  1297.0 5.5 fusion.193
  1328.6 5.5 fusion.193
  1360.1 5.5 fusion.193
  1368.0 5.6 all-to-all-start.3
  1378.5 5.3 broadcast.452.clone2
  1383.8 236.9 %while.30 = (s32[]{:T(128)}, bf16[1,4096,4,256]{3,2,0,1:T(4,128)(2,1)}, bf16[1,6144,256]{2,1,0:T(8,128)(2,1)}, s32[1,4096]{1,0:T(1,128)S(1)}, s32[1,6144]{1,0:T(...) while((s32[]{:T(128)}, ...), condition=%wide.region_4.5_spmd, body=%wide.region_1.4_spmd.sunk | while | flops 1150455168 | bytes 17770988 | solution.py:52
  1625.2 5.7 all-to-all-start.1
  1630.9 15.8 copy.68
  1646.7 9.5 slice.65
  1662.5 9.6 fusion.69
  1672.1 43.3 %fusion.137 = f32[1024,4096]{1,0:T(8,128)} fusion(bf16[1024,4096]{0,1:T(8,128)(2,1)} %bitcast.255, bf16[4096,4096]{1,0:T(8,128)(2,1)} %param.19), kind=kOutput, calls=%fused_computation.180 | convolution fusion | flops 34359738368 | bytes 58720256 | tf_op jit(solution)/shard_map/bcn,dn->bcd/dot_general | solution.py:98
  1715.4 48.2 %fusion.78 = f32[4096,4096]{1,0:T(8,128)} fusion(bf16[1024,4096]{0,1:T(8,128)(2,1)} %bitcast.256, bf16[1,1024,4096]{2,1,0:T(8,128)(2,1)} %param.14, f32[4096]{0:T(1024)S(1)} %copy-done.12, f32[1024]{0:T(1024)S(1)} %copy-done.14), kind=kOutput, calls=%fused_computation.114 | convolution fusion | flops 34376515584 | bytes 83906560 | tf_op jit(solution)/shard_map/bcd,bcn->dn/dot_general | solution.py:101
  1763.5 7.9 copy.62
  1771.4 11.4 copy.63
  1782.8 44.3 %fusion.71 = f32[4096,4096]{1,0:T(8,128)} fusion(bf16[1024,4096]{0,1:T(8,128)(2,1)} %bitcast.258, bf16[1,1024,4096]{2,1,0:T(8,128)(2,1)} %param.17), kind=kOutput, calls=%fused_computation.107 | convolution fusion | flops 34359738368 | bytes 83886080 | tf_op jit(solution)/shard_map/bcn,bcd->nd/dot_general | solution.py:128
  1827.1 39.9 fusion.66
  1869.8 8.9 fusion.80
  1878.7 8.6 fusion.76
  1887.3 8.6 fusion.95
  1895.9 17.6 fusion.61
  1913.5 12.6 convert_reduce_fusion
  1926.2 2388.5 %all-reduce.5 = (bf16[4096]{0:T(1024)(128)(2,1)}, bf16[4096,4096]{1,0:T(8,128)(2,1)}, bf16[4096,256]{1,0:T(8,128)(2,1)}, bf16[4096,256]{1,0:T(8,128)(2,1)}, bf16...) all-reduce(f32[4096]{0:T(1024)S(1)} %get-tuple-element.375, ...), channel_id=1, replica_groups=mesh['dp'=2,'sp'=4] {'sp'}, use_global_device_ids=true, to_apply=%region_14.15 | all-reduce | flops 35659776 | bytes 213958656 | tf_op jit(solution)/shard_map/psum | solution.py:136
  (1155 shorter events, 1131.0 us)
Async XLA Ops:
  7.2 202.0 %copy-start = (bf16[4096,256]{1,0:T(8,128)(2,1)S(1)}, bf16[4096,256]{1,0:T(8,128)(2,1)}, u32[]{:S(2)}) copy-start(bf16[4096,256]{1,0:T(8,128)(2,1)} %param.21) | copy-start | bytes 6291460
  7.2 5.3 copy-start.27
  7.2 5.4 copy-start.21
  7.2 308.4 %all-gather.7.cloned.1.call-start = ((), (), s32[]{:S(2)}) async-start(), calls=%async_computation.9 | async-start | bytes 2621440 | tf_op jit(solution)/shard_map/all_gather | solution.py:120
  7.2 5.9 copy-start.4
  7.3 10.4 copy-start.23
  12.5 5.1 copy-start.18
  12.5 196.6 %copy-start.13 = (f32[1024]{0:T(1024)}, f32[1024]{0:T(1024)S(1)}, u32[]{:S(2)}) copy-start(f32[1024]{0:T(1024)S(1)} %fusion.126) | copy-start | bytes 12292
  12.6 5.1 copy-start.15
  13.1 196.0 %copy-start.11 = (f32[4096]{0:T(1024)}, f32[4096]{0:T(1024)S(1)}, u32[]{:S(2)}) copy-start(f32[4096]{0:T(1024)S(1)} %convert_add_fusion.2) | copy-start | bytes 49156
  94.7 108.6 %all-to-all-start.2 = ((bf16[1,1024,16,256]{3,1,0,2:T(8,128)(2,1)}), bf16[1,1024,16,256]{3,1,0,2:T(8,128)(2,1)}, u32[]{:S(2)}, u32[]{:S(2)}) async-start(bf16[1,1024,16,256]{3,1,0,2:T(8,128)(2,1)} %copy.64), calls=%async_computation.2 | async-start | bytes 16777216 | tf_op jit(solution)/shard_map/all_to_all | solution.py:130
  203.4 130.7 %all-to-all-start = ((bf16[1,1024,16,256]{1,3,0,2:T(8,128)(2,1)}), bf16[1,1024,16,256]{1,3,0,2:T(8,128)(2,1)}, u32[]{:S(2)}, u32[]{:S(2)}) async-start(bf16[1,1024,16,256]{1,3,0,2:T(8,128)(2,1)} %fusion.70), calls=%async_computation | async-start | bytes 16777216 | tf_op jit(solution)/shard_map/all_to_all | solution.py:119
  209.1 6.7 copy-start.22
  209.1 7.3 copy-start.26
  209.1 110.6 %all-gather.5.cloned.1.call-start = ((), (), s32[]{:S(2)}) async-start(), calls=%async_computation.8 | async-start | bytes 2621440 | tf_op jit(solution)/shard_map/all_gather | solution.py:121
  381.2 5.6 copy-start.3
  412.8 5.6 copy-start.3
  444.4 5.5 copy-start.3
  476.0 5.5 copy-start.3
  507.5 5.5 copy-start.3
  539.1 5.5 copy-start.3
  570.6 5.5 copy-start.3
  602.1 5.5 copy-start.3
  633.7 5.5 copy-start.3
  665.2 5.5 copy-start.3
  696.7 5.5 copy-start.3
  728.2 5.5 copy-start.3
  759.7 5.5 copy-start.3
  791.3 5.5 copy-start.3
  822.8 5.5 copy-start.3
  854.4 5.5 copy-start.3
  886.0 5.6 copy-start.3
  917.5 5.6 copy-start.3
  949.1 5.6 copy-start.3
  980.7 5.6 copy-start.3
  1012.4 5.6 copy-start.3
  1044.0 5.6 copy-start.3
  1075.7 5.6 copy-start.3
  1107.3 5.6 copy-start.3
  1139.0 5.6 copy-start.3
  1170.6 5.6 copy-start.3
  1202.2 5.6 copy-start.3
  1233.8 5.6 copy-start.3
  1265.4 5.6 copy-start.3
  1297.0 5.5 copy-start.3
  1328.6 5.5 copy-start.3
  1360.1 5.5 copy-start.3
  1368.0 257.2 %all-to-all-start.3 = ((bf16[1,4096,4,256]{3,2,0,1:T(4,128)(2,1)}), bf16[1,4096,4,256]{3,2,0,1:T(4,128)(2,1)}, u32[]{:S(2)}, u32[]{:S(2)}) async-start(bf16[1,4096,4,256]{3,2,0,1:T(4,128)(2,1)} %get-tuple-element.304), calls=%async_computation.3 | async-start | bytes 16777216 | tf_op jit(solution)/shard_map/all_to_all | solution.py:134
  1373.6 493.4 %reduce-scatter.3.cloned.1.call-start = ((), (), s32[]{:S(2)}) async-start(), calls=%async_computation.6 | async-start | bytes 5242880 | tf_op jit(solution)/shard_map/reduce_scatter | solution.py:132
  1378.3 491.5 %reduce-scatter.5.cloned.1.call-start = ((), (), s32[]{:S(2)}) async-start(), calls=%async_computation.7 | async-start | bytes 5242880 | tf_op jit(solution)/shard_map/reduce_scatter | solution.py:133
  1625.2 138.3 %all-to-all-start.1 = ((bf16[1,4096,4,256]{3,2,0,1:T(4,128)(2,1)}), bf16[1,4096,4,256]{3,2,0,1:T(4,128)(2,1)}, u32[]{:S(2)}, u32[]{:S(2)}) async-start(bf16[1,4096,4,256]{3,2,0,1:T(4,128)(2,1)} %get-tuple-element.303), calls=%async_computation.1 | async-start | bytes 16777216 | tf_op jit(solution)/shard_map/all_to_all | solution.py:125
  1630.9 25.3 copy-start.8
  1630.9 25.3 copy-start.10
  1646.7 11.2 copy-start.5
  1672.1 43.3 %copy-start.12 = (f32[4096]{0:T(1024)S(1)}, f32[4096]{0:T(1024)}, u32[]{:S(2)}) copy-start(f32[4096]{0:T(1024)} %copy-done.11) | copy-start | bytes 49156
  1672.1 43.3 %copy-start.14 = (f32[1024]{0:T(1024)S(1)}, f32[1024]{0:T(1024)}, u32[]{:S(2)}) copy-start(f32[1024]{0:T(1024)} %copy-done.13) | copy-start | bytes 12292
  1782.8 44.3 %copy-start.6 = (bf16[1,1024,4,4,256]{1,4,3,2,0:T(8,128)(2,1)S(1)}, bf16[1,1024,4,4,256]{1,4,3,2,0:T(8,128)(2,1)}, u32[]{:S(2)}) copy-start(bf16[1,1024,4,4,256]{1,4,3,2,0:T(8,128)(2,1)} %copy.63) | copy-start | bytes 25165828
  1782.8 44.3 %copy-start.20 = (f32[4096]{0:T(1024)S(1)}, f32[4096]{0:T(1024)}, u32[]{:S(2)}) copy-start(f32[4096]{0:T(1024)} %convert_element_type.213) | copy-start | bytes 49156
  1827.1 41.3 copy-start.17
  1827.1 41.3 copy-start.25
  1869.8 26.1 slice-start
  1878.7 8.6 copy-start.9
  1878.7 17.2 slice-start.1
  1895.9 17.6 copy-start.19
  (67 other events, 190.9 us)
Sparse Core Ops, SparseCore 0:
  19.8 22.3 all-gather.6
  215.9 34.3 all-gather.4
  1378.4 64.1 reduce-scatter.2
  1625.3 64.9 reduce-scatter.4
where the time goes:
time: 4340 us; the launch traced here: 4320 us
  blocking collectives  2490 us (57%)
  matrix products  980 us (23%)
  local copies, waits for them, and re-layouts  598 us (14%)
  other arithmetic  215 us (5%)
    psum x1, blocking collectives, local_step(): lax.psum((gain_part, w_q_part, w_k_part, w_v_part, w_o_part, b_o_part), '...  2390 us
    dynamic_slice x64, local copies, waits for them, and re-layouts, block_step(): lax.dynamic_slice_in_dim(dk_acc, q_start, key_span, axis=1) + dk_blk  198 us
    dot_general x32, matrix products, block_step(): jnp.einsum('bhqk,bqhe->bke', attn_prob.astype(jnp.bfloat16), do_blk, pref...  178 us
    dynamic_update_slice x64, local copies, waits for them, and re-layouts, block_step(): lax.dynamic_update_slice_in_dim(dk_acc, lax.dynamic_slice_in_dim(dk_acc,...  145 us
    dot_general x64, matrix products, block_probs(): jnp.einsum('bqhe,bke->bhqk', q_blk, k_blk, preferred_element_type=jnp.flo...  133 us
    dot_general x32, matrix products, block_step(): jnp.einsum('bqhe,bke->bhqk', do_blk, v_blk, preferred_element_type=jnp.fl...  105 us
    dot_general x32, matrix products, block_step(): jnp.einsum('bhqk,bqhe->bke', d_score, q_blk, preferred_element_type=jnp.f...  99.9 us
    all_gather x1, blocking collectives, local_step(): seg_all = lax.all_gather(seg_ids, 'sp', axis=1, tiled=True)  99.2 us
  transfers between devices with their start and end apart: 8, of which 0 were waited for; matrix products, arithmetic and copies ran while one was open for 16% of the time, Pallas kernels for 0%

commit v1 on v0

v1 whole, which is shorter than its diff:
```python
import functools

import jax
import jax.numpy as jnp
from jax import lax
from jax.experimental import pallas as pl
from jax.experimental.pallas import tpu as pltpu
from jax.sharding import PartitionSpec as P

WINDOW = 2048
NORM_EPS = 1e-6
ROPE_BASE = 10000.0
NEG_BIG = -1e30
POS_BIG = 3e38
HEAD_DIM = 256
ROT_HALF = HEAD_DIM // 4

FWD_BQ, FWD_BK, FWD_G = 256, 512, 4
BWD_BQ, BWD_BK, BWD_G = 256, 512, 4

NT = (((1,), (1,)), ((), ()))
NN = (((1,), (0,)), ((), ()))


def dot(a, b, dims):
    return lax.dot_general(a, b, dims, preferred_element_type=jnp.float32)


def rms_norm(x_f32, gain_f32):
    mean_sq = jnp.mean(x_f32 * x_f32, axis=-1, keepdims=True)
    return (x_f32 * lax.rsqrt(mean_sq + NORM_EPS) * (1.0 + gain_f32)).astype(jnp.bfloat16)


def rope_tables(positions):
    rot_dim = 2 * ROT_HALF
    inv_freq = ROPE_BASE ** (-(jnp.arange(ROT_HALF, dtype=jnp.float32) * 2.0 / rot_dim))
    angles = positions.astype(jnp.float32)[:, None] * inv_freq
    return jnp.cos(angles), jnp.sin(angles)


def rotary(vals, cos_a, sin_a):
    a = vals[..., :ROT_HALF]
    b = vals[..., ROT_HALF:2 * ROT_HALF]
    cos_a, sin_a = cos_a[:, None, :], sin_a[:, None, :]
    return jnp.concatenate([a * cos_a - b * sin_a, b * cos_a + a * sin_a, vals[..., 2 * ROT_HALF:]], axis=-1)


def key_cap(k0, first_key, own_key, bk, bq):
    key_idx = k0 + lax.broadcasted_iota(jnp.int32, (bk, bq), 0)
    return jnp.where((key_idx >= first_key) & (key_idx <= own_key), POS_BIG, NEG_BIG)


def fwd_kernel(bq, bk, group, lo_ref, hi_ref, t0_ref, q_ref, k_ref, vt_ref, first_ref, o_ref, lse_ref, m_s, l_s, acc_s):
    i = pl.program_id(0)
    first_key = first_ref[0]
    own_key = t0_ref[i] + lax.broadcasted_iota(jnp.int32, (1, bq), 1)
    m_s[...] = jnp.full_like(m_s, NEG_BIG)
    l_s[...] = jnp.zeros_like(l_s)
    acc_s[...] = jnp.zeros_like(acc_s)

    def body(j, carry):
        k0 = pl.multiple_of(j * bk, bk)
        k_blk = k_ref[pl.ds(k0, bk), :]
        vt_blk = vt_ref[:, pl.ds(k0, bk)]
        cap = key_cap(k0, first_key, own_key, bk, bq)
        for h in range(group):
            s = jnp.minimum(dot(k_blk, q_ref[:, h * HEAD_DIM:(h + 1) * HEAD_DIM], NT), cap)
            m_old = m_s[h:h + 1]
            m_new = jnp.maximum(m_old, jnp.max(s, axis=0, keepdims=True))
            p = jnp.exp(s - m_new)
            alpha = jnp.exp(m_old - m_new)
            l_s[h:h + 1] = l_s[h:h + 1] * alpha + jnp.sum(p, axis=0, keepdims=True)
            m_s[h:h + 1] = m_new
            acc_s[h] = acc_s[h] * alpha + dot(vt_blk, p.astype(jnp.bfloat16), NN)
        return carry

    lax.fori_loop(lo_ref[i], hi_ref[i], body, 0)
    for h in range(group):
        l_h = l_s[h:h + 1]
        o_ref[:, h * HEAD_DIM:(h + 1) * HEAD_DIM] = (acc_s[h] / l_h).T.astype(jnp.bfloat16)
        lse_ref[0, 0, h:h + 1] = m_s[h:h + 1] + jnp.log(l_h)


def block_bounds(first_key, t0, bq, bk):
    blk_first = first_key.reshape(-1, bq)[:, 0]
    starts = t0 + jnp.arange(first_key.shape[0] // bq, dtype=jnp.int32) * bq
    return blk_first // bk, (starts + bq - 1) // bk + 1, starts


def attn_fwd(q, k, vt, first_key, t0):
    bq, bk, group = FWD_BQ, FWD_BK, FWD_G
    tokens, width = q.shape
    seq = k.shape[0]
    nq, ng = tokens // bq, width // (group * HEAD_DIM)
    lo, hi, starts = block_bounds(first_key, t0, bq, bk)
    o, lse = pl.pallas_call(
        functools.partial(fwd_kernel, bq, bk, group),
        grid_spec=pltpu.PrefetchScalarGridSpec(
            num_scalar_prefetch=3, grid=(nq, ng),
            in_specs=[pl.BlockSpec((bq, group * HEAD_DIM), lambda i, g, *_: (i, g)),
                      pl.BlockSpec((seq, HEAD_DIM), lambda i, g, *_: (0, 0)),
                      pl.BlockSpec((HEAD_DIM, seq), lambda i, g, *_: (0, 0)),
                      pl.BlockSpec((1, 1, bq), lambda i, g, *_: (i, 0, 0))],
            out_specs=[pl.BlockSpec((bq, group * HEAD_DIM), lambda i, g, *_: (i, g)),
                       pl.BlockSpec((1, 1, group, bq), lambda i, g, *_: (i, g, 0, 0))],
            scratch_shapes=[pltpu.VMEM((group, bq), jnp.float32), pltpu.VMEM((group, bq), jnp.float32),
                            pltpu.VMEM((group, HEAD_DIM, bq), jnp.float32)]),
        out_shape=[jax.ShapeDtypeStruct(q.shape, jnp.bfloat16),
                   jax.ShapeDtypeStruct((nq, ng, group, bq), jnp.float32)],
        compiler_params=pltpu.CompilerParams(dimension_semantics=("arbitrary", "arbitrary")),
        cost_estimate=pl.CostEstimate(flops=4 * tokens * width * 1024, bytes_accessed=4 * tokens * width, transcendentals=0),
        name="attn_fwd",
    )(lo, hi, starts, q, k, vt, first_key.reshape(nq, 1, bq))
    return o, lse


def bwd_kernel(bq, bk, group, lo_ref, hi_ref, t0_ref, q_ref, do_ref, o_ref, lse_ref, first_ref, cos_ref, sin_ref,
               k_ref, kt_ref, v_ref, dk_in, dv_in, dq_ref, dk_ref, dv_ref, dq_s, delta_s):
    i = pl.program_id(0)

    @pl.when((i == 0) & (pl.program_id(1) == 0))
    def _():
        dk_ref[...] = dk_in[...]
        dv_ref[...] = dv_in[...]

    first_key = first_ref[0]
    own_key = t0_ref[i] + lax.broadcasted_iota(jnp.int32, (1, bq), 1)
    dq_s[...] = jnp.zeros_like(dq_s)
    for h in range(group):
        cols = slice(h * HEAD_DIM, (h + 1) * HEAD_DIM)
        row_dot = jnp.sum(do_ref[:, cols].astype(jnp.float32) * o_ref[:, cols].astype(jnp.float32), axis=1, keepdims=True)
        delta_s[h:h + 1] = jnp.broadcast_to(row_dot, (bq, 128)).T[0:1]

    def body(j, carry):
        k0 = pl.multiple_of(j * bk, bk)
        k_blk = k_ref[pl.ds(k0, bk), :]
        v_blk = v_ref[pl.ds(k0, bk), :]
        kt_blk = kt_ref[:, pl.ds(k0, bk)]
        cap = key_cap(k0, first_key, own_key, bk, bq)
        p_all, ds_all = [], []
        for h in range(group):
            cols = slice(h * HEAD_DIM, (h + 1) * HEAD_DIM)
            s = jnp.minimum(dot(k_blk, q_ref[:, cols], NT), cap)
            p = jnp.exp(s - lse_ref[0, 0, h:h + 1])
            dp = dot(v_blk, do_ref[:, cols], NT)
            ds = (p * (dp - delta_s[h:h + 1])).astype(jnp.bfloat16)
            p_all.append(p.astype(jnp.bfloat16))
            ds_all.append(ds)
            dq_s[h] += dot(kt_blk, ds, NN)
        q_rows = jnp.concatenate([q_ref[:, h * HEAD_DIM:(h + 1) * HEAD_DIM] for h in range(group)], axis=0)
        do_rows = jnp.concatenate([do_ref[:, h * HEAD_DIM:(h + 1) * HEAD_DIM] for h in range(group)], axis=0)
        dv_ref[pl.ds(k0, bk), :] += dot(jnp.concatenate(p_all, axis=1), do_rows, NN)
        dk_ref[pl.ds(k0, bk), :] += dot(jnp.concatenate(ds_all, axis=1), q_rows, NN)
        return carry

    lax.fori_loop(lo_ref[i], hi_ref[i], body, 0)
    cos_t, sin_t = cos_ref[...], sin_ref[...]
    for h in range(group):
        dq = dq_s[h].astype(jnp.bfloat16).astype(jnp.float32)
        a, b = dq[:ROT_HALF], dq[ROT_HALF:2 * ROT_HALF]
        dq_lin = jnp.concatenate([a * cos_t + b * sin_t, b * cos_t - a * sin_t, dq[2 * ROT_HALF:]], axis=0) * HEAD_DIM ** -0.5
        dq_ref[:, h * HEAD_DIM:(h + 1) * HEAD_DIM] = dq_lin.T.astype(jnp.bfloat16)


def attn_bwd(q, d_o, o, lse, k, kt, v, first_key, t0, cos_a, sin_a, dk_in, dv_in):
    bq, bk, group = BWD_BQ, BWD_BK, BWD_G
    tokens, width = q.shape
    seq = k.shape[0]
    nq, ng = tokens // bq, width // (group * HEAD_DIM)
    lo, hi, starts = block_bounds(first_key, t0, bq, bk)
    tile = pl.BlockSpec((bq, group * HEAD_DIM), lambda i, g, *_: (i, g))
    whole = pl.BlockSpec((seq, HEAD_DIM), lambda i, g, *_: (0, 0))
    trig = pl.BlockSpec((ROT_HALF, bq), lambda i, g, *_: (0, i))
    acc_shape = jax.ShapeDtypeStruct((seq, HEAD_DIM), jnp.float32)
    return pl.pallas_call(
        functools.partial(bwd_kernel, bq, bk, group),
        grid_spec=pltpu.PrefetchScalarGridSpec(
            num_scalar_prefetch=3, grid=(nq, ng),
            in_specs=[tile, tile, tile,
                      pl.BlockSpec((1, 1, group, bq), lambda i, g, *_: (i, g, 0, 0)),
                      pl.BlockSpec((1, 1, bq), lambda i, g, *_: (i, 0, 0)),
                      trig, trig, whole, pl.BlockSpec((HEAD_DIM, seq), lambda i, g, *_: (0, 0)), whole, whole, whole],
            out_specs=[tile, whole, whole],
            scratch_shapes=[pltpu.VMEM((group, HEAD_DIM, bq), jnp.float32), pltpu.VMEM((group, bq), jnp.float32)]),
        out_shape=[jax.ShapeDtypeStruct(q.shape, jnp.bfloat16), acc_shape, acc_shape],
        compiler_params=pltpu.CompilerParams(dimension_semantics=("arbitrary", "arbitrary"), vmem_limit_bytes=60 * 2 ** 20),
        cost_estimate=pl.CostEstimate(flops=10 * tokens * width * 1024, bytes_accessed=8 * tokens * width, transcendentals=0),
        name="attn_bwd",
    )(lo, hi, starts, q, d_o, o, lse, first_key.reshape(nq, 1, bq), cos_a.T, sin_a.T, k, kt, v, dk_in, dv_in)


def solution(mesh):
    row_spec = P("dp", "sp", None)
    tok_spec = P("dp", "sp")
    mat_spec = P(None, None)
    grad_mat = P("dp", None)
    chips_perm = [(0, 2), (1, 3), (2, 0), (3, 1)]
    cores_perm = [(0, 1), (1, 0), (2, 3), (3, 2)]

    def to_chip(val):
        return lax.ppermute(val, "sp", chips_perm)

    def to_core(val):
        return lax.ppermute(val, "sp", cores_perm)

    def by_core(core, mine, theirs, axis):
        first = jnp.where(core == 0, mine, theirs)
        second = jnp.where(core == 0, theirs, mine)
        return jnp.concatenate([first, second], axis=axis)

    def local_step(x, seg_ids, positions, out_grad, norm_scale, w_q, w_k, w_v, w_o, b_o):
        x, out_grad = x[0], out_grad[0]
        chunk, dim = x.shape
        me = lax.axis_index("sp")
        core = me % 2
        half = w_q.shape[1] // 2
        pieces = [me, me ^ 1, me ^ 2, me ^ 3]

        meta = lax.all_gather(jnp.stack([seg_ids[0], positions[0]]), "sp", axis=1, tiled=True)
        seg_all, pos_all = meta[0], meta[1]
        seq = seg_all.shape[0]
        token = jnp.arange(seq, dtype=jnp.int32)
        is_start = jnp.concatenate([jnp.ones((1,), jnp.bool_), seg_all[1:] != seg_all[:-1]])
        doc_start = lax.cummax(jnp.where(is_start, token, 0))
        first_key_all = jnp.maximum(doc_start, token - (WINDOW - 1))
        cos_all, sin_all = rope_tables(pos_all)

        def piece_rows(val, piece):
            return lax.dynamic_slice_in_dim(val, piece * chunk, chunk, axis=0)

        x_f32 = x.astype(jnp.float32)
        n_own, norm_pull = jax.vjp(rms_norm, x_f32, norm_scale.astype(jnp.float32))

        w_kv = jnp.concatenate([w_k, w_v], axis=1)
        kv_lin = dot(n_own, w_kv, NN)
        cos_own, sin_own = piece_rows(cos_all, me), piece_rows(sin_all, me)
        k_own = rotary(kv_lin[:, None, :HEAD_DIM], cos_own, sin_own)[:, 0].astype(jnp.bfloat16)
        kv_own = jnp.concatenate([k_own, kv_lin[:, HEAD_DIM:].astype(jnp.bfloat16)], axis=1)
        kv_1 = to_core(kv_own)
        kv_2 = to_chip(kv_own)
        kv_3 = to_core(kv_2)
        kv_all = jnp.zeros((seq, 2 * HEAD_DIM), jnp.bfloat16)
        for piece, val in zip(pieces, (kv_own, kv_1, kv_2, kv_3)):
            kv_all = lax.dynamic_update_slice_in_dim(kv_all, val, piece * chunk, axis=0)
        k_all, v_all = kv_all[:, :HEAD_DIM], kv_all[:, HEAD_DIM:]
        kt_all, vt_all = k_all.T, v_all.T

        n_1 = to_core(n_own)
        n_2 = to_chip(n_own)
        n_3 = to_core(n_2)
        g_1 = to_core(out_grad)
        g_2 = to_chip(out_grad)
        g_3 = to_core(g_2)
        n_all = [n_own, n_1, n_2, n_3]
        g_all = [out_grad, g_1, g_2, g_3]

        w_q_half = lax.dynamic_slice_in_dim(w_q, core * half, half, axis=1)
        w_o_half = lax.dynamic_slice_in_dim(w_o, core * half, half, axis=0)

        o_all, dq_all = [], []
        dk = jnp.zeros((seq, HEAD_DIM), jnp.float32)
        dv = jnp.zeros((seq, HEAD_DIM), jnp.float32)
        for p in range(4):
            first_key = piece_rows(first_key_all, pieces[p])
            cos_p, sin_p = piece_rows(cos_all, pieces[p]), piece_rows(sin_all, pieces[p])
            q_lin = dot(n_all[p], w_q_half, NN).reshape(chunk, -1, HEAD_DIM)
            q = (rotary(q_lin, cos_p, sin_p) * HEAD_DIM ** -0.5).astype(jnp.bfloat16).reshape(chunk, half)
            o, lse = attn_fwd(q, k_all, vt_all, first_key, pieces[p] * chunk)
            d_o = dot(g_all[p], w_o_half, NT).astype(jnp.bfloat16)
            dq, dk, dv = attn_bwd(q, d_o, o, lse, k_all, kt_all, v_all, first_key, pieces[p] * chunk, cos_p, sin_p, dk, dv)
            o_all.append(o)
            dq_all.append(dq)

        o_tok = by_core(core, o_all[0], to_core(o_all[1]), 1)
        block_out = (x_f32 + dot(o_tok, w_o, NN) + b_o.astype(jnp.float32)).astype(jnp.bfloat16)

        TN = (((0,), (0,)), ((), ()))
        w_o_part = sum(dot(o_all[p], g_all[p], TN) for p in range(4)).astype(jnp.bfloat16)
        w_q_part = sum(dot(n_all[p], dq_all[p], TN) for p in range(4)).astype(jnp.bfloat16)
        w_o_grad = by_core(core, w_o_part, to_core(w_o_part), 0)
        w_q_grad = by_core(core, w_q_part, to_core(w_q_part), 1)

        dkv = jnp.concatenate([dk, dv], axis=1)
        dkv = dkv + to_core(dkv)
        dk_lin = rotary(dkv[:, None, :HEAD_DIM].astype(jnp.bfloat16).astype(jnp.float32), cos_all, -sin_all)[:, 0].astype(jnp.bfloat16)
        dkv_lin = jnp.concatenate([dk_lin, dkv[:, HEAD_DIM:].astype(jnp.bfloat16)], axis=1)
        w_kv_grad = sum(dot(n_all[p], piece_rows(dkv_lin, pieces[p]), TN) for p in range(4)).astype(jnp.bfloat16)

        dq_tok = by_core(core, dq_all[0], to_core(dq_all[1]), 1)
        d_normed = (dot(dq_tok, w_q, NT) + dot(piece_rows(dkv_lin, me), w_kv, NT)).astype(jnp.bfloat16)
        dx_norm, gain_part = norm_pull(d_normed)
        x_grad = (out_grad.astype(jnp.float32) + dx_norm).astype(jnp.bfloat16)
        b_o_part = jnp.sum(out_grad, axis=0, dtype=jnp.float32)
        sums = lax.psum(jnp.stack([gain_part, b_o_part]), "sp").astype(jnp.bfloat16)
        return (block_out[None], x_grad[None], sums[0], w_q_grad, w_kv_grad[:, :HEAD_DIM], w_kv_grad[:, HEAD_DIM:], w_o_grad, sums[1])

    return jax.shard_map(local_step, mesh=mesh,
                         in_specs=(row_spec, tok_spec, tok_spec, row_spec, P(None), mat_spec, mat_spec, mat_spec, mat_spec, P(None)),
                         out_specs=(row_spec, row_spec, P("dp"), grad_mat, grad_mat, grad_mat, grad_mat, P("dp")),
                         check_vma=False)
```

time: 4340 us -> 1320 us (0.30)
  blocking collectives: 2490 us -> 20.8 us
  local copies, waits for them, and re-layouts: 598 us -> 145 us
  matrix products: 980 us -> 577 us
  Pallas kernels: 0 us -> 363 us
    psum x1, blocking collectives: 2390 us -> 10.5 us  [local_step(): sums = lax.psum(jnp.stack([gain_part, b_o_part]), 'sp').astype(jnp.bfloat16)]
    dot_general x236 -> x24, matrix products: 980 us -> 577 us  [dot(): return lax.dot_general(a, b, dims, preferred_element_type=jnp.float32)]
    pallas_call x0 -> x8, Pallas kernels: none -> 363 us  [the longest x4 223 us: attn_bwd(): pl.pallas_call(functools.partial(bwd_kernel, bq, bk, group), grid_spec=pl...]
    dynamic_update_slice x192 -> x3, local copies, waits for them, and re-layouts: 208 us -> 3.13 us  [local_step(): kv_all = lax.dynamic_update_slice_in_dim(kv_all, val, piece * chunk, axis=0)]
    dynamic_slice x128 -> x4, local copies, waits for them, and re-layouts: 200 us -> 1.58 us  [piece_rows(): return lax.dynamic_slice_in_dim(val, piece * chunk, chunk, axis=0)]
    and x64 -> x0, other arithmetic: 94.9 us -> none  [block_probs(): allowed = (q_seg[:, :, None] == k_seg[:, None, :]) & in_band[None]]
    all_gather x1, blocking collectives: 99.2 us -> 10.3 us  [local_step(): lax.all_gather(jnp.stack([seg_ids[0], positions[0]]), 'sp', axis=1, tiled...]
    select_n x0 -> x9, other arithmetic: none -> 55 us  [the longest x4 52.7 us: by_core(): first = jnp.where(core == 0, mine, theirs)]
  transfers between devices with their start and end apart: 8 -> 14, of which waited for: 0 -> 0; matrix products, arithmetic and copies ran while one was open for 16% -> 59% of each run, Pallas kernels for 0% -> 24%
where the time goes in v1:
time: 1320 us; the launch traced here: 1330 us
  matrix products  577 us (44%)
  Pallas kernels  363 us (28%)
  other arithmetic  178 us (13%)
  local copies, waits for them, and re-layouts  145 us (11%)
  starting transfers between devices  44.1 us (3%)
  blocking collectives  20.8 us (2%)
    dot_general x24, matrix products, dot(): return lax.dot_general(a, b, dims, preferred_element_type=jnp.float32)  577 us
    pallas_call x4, Pallas kernels, attn_bwd(): pl.pallas_call(functools.partial(bwd_kernel, bq, bk, group), grid_spec=pl...  223 us
    pallas_call x4, Pallas kernels, attn_fwd(): pl.pallas_call(functools.partial(fwd_kernel, bq, bk, group), grid_spec=pl...  140 us
    select_n x4, other arithmetic, by_core(): first = jnp.where(core == 0, mine, theirs)  52.7 us
    unnamed x85, local copies, waits for them, and re-layouts  50.2 us
    concatenate x2, other arithmetic, by_core(): return jnp.concatenate([first, second], axis=axis)  47.5 us
    ppermute x11, starting transfers between devices, to_core(): return lax.ppermute(val, 'sp', cores_perm)  41.8 us
    dot_general x2, local copies, waits for them, and re-layouts, dot(): return lax.dot_general(a, b, dims, preferred_element_type=jnp.float32)  35.4 us
  transfers between devices with their start and end apart: 14, of which 0 were waited for; matrix products, arithmetic and copies ran while one was open for 59% of the time, Pallas kernels for 24%

profile of v1, /device:TPU:0, one launch (start us, length us, event | category | flops | bytes accessed | tf_op | source)
XLA Modules:
  0.0 1330.3 jit_solution(8365216936190219314)
XLA Ops:
  0.7 5.2 fusion.10
  6.7 11.9 fusion.7
  18.6 6.9 fusion.119
  25.8 10.3 all_gather.3
  36.1 3.7 multiply_cosine_fusion.1
  50.6 24.3 %convert_bitcast_fusion.4.do_ref = bf16[1024,2048]{1,0:T(8,128)(2,1)} fusion(bf16[4096,4096]{1,0:T(8,128)(2,1)} %param.18, s32[]{:T(128)S(6)} %select_n.131, bf16[1,1024,4096]{2,1,0:T(8,128)(2,1)} %param.13), kind=kOutput, calls=%fused_computation.82 | convolution fusion | flops 17181966336 | bytes 29360132 | tf_op jit(solution)/shard_map/dot_general | solution.py:26
  74.9 14.2 %dynamic-slice_bitcast_fusion = bf16[2048,4096]{0,1:T(8,128)(2,1)} fusion(bf16[4096,4096]{1,0:T(8,128)(2,1)} %param.15, s32[]{:T(128)S(6)} %select_n.131), kind=kLoop, calls=%fused_computation.46 | loop fusion | bytes 33554436 | tf_op jit(solution)/shard_map/dot_general | solution.py:26
  89.1 21.2 %copy.93 = bf16[2048,4096]{1,0:T(8,128)(2,1)} copy(bf16[2048,4096]{0,1:T(8,128)(2,1)} %dynamic-slice_bitcast_fusion) | data formatting | bytes 33554432 | tf_op jit(solution)/shard_map/dot_general | solution.py:26
  110.3 22.4 %fusion.31 = f32[1024,8,256]{0,2,1:T(8,128)S(1)} fusion(bf16[8,256,4096]{2,1,0:T(8,128)(2,1)} %bitcast.157, bf16[1,1024,4096]{2,1,0:T(8,128)(2,1)} %param.10, f32[4096]{0:T(1024)S(1)} %convert_add_fusion.1, f32[1024]{0:T(1024)S(1)} %fusion.93), kind=kOutput, calls=%fused_computation.48 | convolution fusion | flops 17196646400 | bytes 33574912 | tf_op jit(solution)/shard_map/dot_general | solution.py:26
  133.6 2.6 fusion.35
  137.4 6.4 copy.127.q_ref
  150.2 5.2 fusion.117
  155.4 4.1 copy.104.kt_ref
  159.5 3.0 copy.99.vt_ref
  162.5 24.5 %attn_fwd.4 = (bf16[1024,2048]{1,0:T(8,128)(2,1)}, f32[4,2,4,256]{3,2,1,0:T(4,128)}) custom-call(s32[4]{0:T(128)} %and_select_fusion.7.lo_ref, s32[4]{0:T(128)} %get-tuple-element.132.hi_ref, s32[4]{0:T(128)} %get-tuple-element.133.t0_ref, bf16[1024,2048]{1,0:T(8,128)(2,1)} %copy.127.q_ref, bf16[4096,256]{1,0:T(8,128)(2,1)} %get-tuple-element.112.k_ref, ...), custom_call_target="tpu_custom_call" | custom-call | flops 8589934592 | bytes 8388608 | tf_op jit(solution)/shard_map/attn_fwd/pallas_call | solution.py:96
  187.0 25.4 %fusion.107 = f32[2048,4096]{1,0:T(8,128)} fusion(bf16[1024,2048]{1,0:T(8,128)(2,1)} %get-tuple-element.28.o_ref, bf16[1,1024,4096]{2,1,0:T(8,128)(2,1)} %param.13), kind=kOutput, calls=%fused_computation.220 | convolution fusion | flops 17179869184 | bytes 46137344 | tf_op jit(solution)/shard_map/dot_general | solution.py:26
  214.7 41.2 %attn_bwd.4 = (bf16[1024,2048]{1,0:T(8,128)(2,1)}, f32[4096,256]{1,0:T(8,128)}, f32[4096,256]{1,0:T(8,128)}) custom-call(s32[4]{0:T(128)} %and_select_fusion.7.lo_ref, s32[4]{0:T(128)} %get-tuple-element.132.hi_ref, s32[4]{0:T(128)} %get-tuple-element.133.t0_ref, bf16[1024,2048]{1,0:T(8,128)(2,1)} %copy.127.q_ref, ...), custom_call_target="tpu_custom_call" | custom-call | flops 21474836480 | bytes 16777216 | tf_op jit(solution)/shard_map/attn_bwd/pallas_call | solution.py:175
  255.9 25.8 %fusion.120 = f32[4096,2048]{0,1:T(8,128)} fusion(bf16[1024,4096]{1,0:T(8,128)(2,1)} %fusion.7, bf16[1024,2048]{1,0:T(8,128)(2,1)} %get-tuple-element.31), kind=kOutput, calls=%fused_computation.233 | convolution fusion | flops 17179869184 | bytes 46137344 | tf_op jit(solution)/shard_map/dot_general | solution.py:26
  281.7 24.2 %fusion.24 = f32[1024,2048]{0,1:T(8,128)} fusion(bf16[1024,4096]{1,0:T(8,128)(2,1)} %collective-permute-done.7, bf16[4096,4096]{1,0:T(8,128)(2,1)} %param.15, s32[]{:T(128)S(6)} %select_n.131), kind=kOutput, calls=%fused_computation.40 | convolution fusion | flops 17179869184 | bytes 33554436 | tf_op jit(solution)/shard_map/dot_general | solution.py:26
  305.9 2.7 slice.190
  308.6 24.4 %fusion.28 = f32[1024,2048]{0,1:T(8,128)} fusion(bf16[1024,4096]{1,0:T(8,128)(2,1)} %collective-permute-done.3, bf16[4096,4096]{1,0:T(8,128)(2,1)} %param.15, s32[]{:T(128)S(6)} %select_n.131), kind=kOutput, calls=%fused_computation.44 | convolution fusion | flops 17179869184 | bytes 33554436 | tf_op jit(solution)/shard_map/dot_general | solution.py:26
  333.1 2.8 multiply_subtract_fusion
  335.9 2.7 fusion.46
  338.6 6.5 copy.130.q_ref
  347.6 2.8 multiply_subtract_fusion.2
  353.0 6.4 copy.128.q_ref
  359.5 48.5 %attn_fwd.5 = (bf16[1024,2048]{1,0:T(8,128)(2,1)}, f32[4,2,4,256]{3,2,1,0:T(4,128)}) custom-call(s32[4]{0:T(128)} %get-tuple-element.134.lo_ref, s32[4]{0:T(128)} %get-tuple-element.135.hi_ref, s32[4]{0:T(128)} %fusion.100.t0_ref, bf16[1024,2048]{1,0:T(8,128)(2,1)} %copy.128.q_ref, bf16[4096,256]{1,0:T(8,128)(2,1)} %get-tuple-element.112.k_ref, ...), custom_call_target="tpu_custom_call" | custom-call | flops 8589934592 | bytes 8388608 | tf_op jit(solution)/shard_map/attn_fwd/pallas_call | solution.py:96
  408.0 33.9 %collective-permute-start.4 = (bf16[1024,2048]{1,0:T(8,128)(2,1)}, bf16[1024,2048]{1,0:T(8,128)(2,1)}, u32[]{:S(2)}, u32[]{:S(2)}) collective-permute-start(bf16[1024,2048]{1,0:T(8,128)(2,1)} %get-tuple-element.29.o_ref), channel_id=1, source_target_pairs={{0,1},{1,0},{2,3},{3,2},{4,5},{5,4},{6,7},{7,6}} | collective-permute-start | bytes 12582920 | tf_op jit(solution)/shard_map/ppermute | solution.py:204
  441.9 24.2 %convert_bitcast_fusion.3.do_ref = bf16[1024,2048]{1,0:T(8,128)(2,1)} fusion(bf16[1024,4096]{1,0:T(8,128)(2,1)} %collective-permute-done.5, bf16[4096,4096]{1,0:T(8,128)(2,1)} %param.18, s32[]{:T(128)S(6)} %select_n.131), kind=kOutput, calls=%fused_computation.81 | convolution fusion | flops 17181966336 | bytes 29360132 | tf_op jit(solution)/shard_map/dot_general | solution.py:26
  466.2 74.6 %attn_bwd.5 = (bf16[1024,2048]{1,0:T(8,128)(2,1)}, f32[4096,256]{1,0:T(8,128)}, f32[4096,256]{1,0:T(8,128)}) custom-call(s32[4]{0:T(128)} %get-tuple-element.134.lo_ref, s32[4]{0:T(128)} %get-tuple-element.135.hi_ref, s32[4]{0:T(128)} %fusion.100.t0_ref, bf16[1024,2048]{1,0:T(8,128)(2,1)} %copy.128.q_ref, bf16[1024,2048]{1,0:T(8,128)(2,1)} %convert_bitcast_fusion.3.do_ref, ...), custom_call_target="tpu_custom_call" | custom-call | flops 21474836480 | bytes 16777216 | tf_op jit(solution)/shard_map/attn_bwd/pallas_call | solution.py:175
  541.3 36.5 %attn_fwd.7 = (bf16[1024,2048]{1,0:T(8,128)(2,1)}, f32[4,2,4,256]{3,2,1,0:T(4,128)}) custom-call(s32[4]{0:T(128)} %and_select_fusion.1.lo_ref, s32[4]{0:T(128)} %get-tuple-element.142.hi_ref, s32[4]{0:T(128)} %get-tuple-element.143.t0_ref, bf16[1024,2048]{1,0:T(8,128)(2,1)} %copy.130.q_ref, bf16[4096,256]{1,0:T(8,128)(2,1)} %get-tuple-element.112.k_ref, ...), custom_call_target="tpu_custom_call" | custom-call | flops 8589934592 | bytes 8388608 | tf_op jit(solution)/shard_map/attn_fwd/pallas_call | solution.py:96
  577.9 24.1 %convert_bitcast_fusion.1.do_ref = bf16[1024,2048]{1,0:T(8,128)(2,1)} fusion(bf16[1024,4096]{1,0:T(8,128)(2,1)} %collective-permute-done.9, bf16[4096,4096]{1,0:T(8,128)(2,1)} %param.18, s32[]{:T(128)S(6)} %select_n.131), kind=kOutput, calls=%fused_computation.79 | convolution fusion | flops 17181966336 | bytes 29360132 | tf_op jit(solution)/shard_map/dot_general | solution.py:26
  601.9 23.4 %fusion.121 = f32[4096,2048]{0,1:T(8,128)} fusion(bf16[1024,4096]{1,0:T(8,128)(2,1)} %collective-permute-done.3, bf16[1024,2048]{1,0:T(8,128)(2,1)S(1)} %copy-done.39), kind=kOutput, calls=%fused_computation.234 | convolution fusion | flops 17179869184 | bytes 46137344 | tf_op jit(solution)/shard_map/dot_general | solution.py:26
  625.3 23.8 %fusion.123 = f32[2048,4096]{1,0:T(8,128)} fusion(bf16[1024,2048]{1,0:T(8,128)(2,1)S(1)} %copy-done.38, bf16[1024,4096]{1,0:T(8,128)(2,1)} %collective-permute-done.5), kind=kOutput, calls=%fused_computation.236 | convolution fusion | flops 17179869184 | bytes 46137344 | tf_op jit(solution)/shard_map/dot_general | solution.py:26
  649.1 23.5 %fusion.124 = f32[2048,4096]{1,0:T(8,128)} fusion(bf16[1024,2048]{1,0:T(8,128)(2,1)S(1)} %copy-done.40, bf16[1024,4096]{1,0:T(8,128)(2,1)} %collective-permute-done.9), kind=kOutput, calls=%fused_computation.237 | convolution fusion | flops 17179869184 | bytes 46137344 | tf_op jit(solution)/shard_map/dot_general | solution.py:26
  672.6 57.7 %attn_bwd.6 = (bf16[1024,2048]{1,0:T(8,128)(2,1)}, f32[4096,256]{1,0:T(8,128)}, f32[4096,256]{1,0:T(8,128)}) custom-call(s32[4]{0:T(128)} %and_select_fusion.1.lo_ref, s32[4]{0:T(128)} %get-tuple-element.142.hi_ref, s32[4]{0:T(128)} %get-tuple-element.143.t0_ref, bf16[1024,2048]{1,0:T(8,128)(2,1)} %copy.130.q_ref, ...), custom_call_target="tpu_custom_call" | custom-call | flops 21474836480 | bytes 16777216 | tf_op jit(solution)/shard_map/attn_bwd/pallas_call | solution.py:175
  730.3 26.2 %fusion.122 = f32[4096,2048]{0,1:T(8,128)} fusion(bf16[1024,4096]{1,0:T(8,128)(2,1)} %collective-permute-done.7, bf16[1024,2048]{1,0:T(8,128)(2,1)} %get-tuple-element.46), kind=kOutput, calls=%fused_computation.235 | convolution fusion | flops 17179869184 | bytes 46137344 | tf_op jit(solution)/shard_map/dot_general | solution.py:26
  759.1 39.7 %fusion.33 = bf16[1,1024,4096]{2,1,0:T(8,128)(2,1)} fusion(bf16[1,1024,4096]{2,1,0:T(8,128)(2,1)} %param.10, f32[4096]{0:T(1024)S(1)} %copy-done.31, bf16[4096,4096]{1,0:T(8,128)(2,1)} %param.18, bf16[1024,2048]{1,0:T(8,128)(2,1)S(1)} %get-tuple-element.101, bf16[1024,2048]{1,0:T(8,128)(2,1)S(1)} %get-tuple-element.100), kind=kOutput, calls=%fused_computation.49 | convolution fusion | flops 34393292800 | bytes 58736640 | tf_op jit(solution)/shard_map/dot_general | solution.py:26
  798.8 5.2 broadcast_select_fusion.5
  804.0 23.1 %fusion.26 = f32[1024,2048]{0,1:T(8,128)S(1)} fusion(bf16[1024,4096]{1,0:T(8,128)(2,1)} %collective-permute-done.8, bf16[4096,4096]{1,0:T(8,128)(2,1)} %param.15, s32[]{:T(128)S(6)} %select_n.131), kind=kOutput, calls=%fused_computation.42 | convolution fusion | flops 17179869184 | bytes 33554436 | tf_op jit(solution)/shard_map/dot_general | solution.py:26
  828.8 2.6 fusion.45
  831.4 6.5 copy.129.q_ref
  837.9 30.5 %attn_fwd.6 = (bf16[1024,2048]{1,0:T(8,128)(2,1)}, f32[4,2,4,256]{3,2,1,0:T(4,128)}) custom-call(s32[4]{0:T(128)} %and_select_fusion.3.lo_ref, s32[4]{0:T(128)} %get-tuple-element.140.hi_ref, s32[4]{0:T(128)} %get-tuple-element.141.t0_ref, bf16[1024,2048]{1,0:T(8,128)(2,1)} %copy.129.q_ref, bf16[4096,256]{1,0:T(8,128)(2,1)} %get-tuple-element.112.k_ref, ...), custom_call_target="tpu_custom_call" | custom-call | flops 8589934592 | bytes 8388608 | tf_op jit(solution)/shard_map/attn_fwd/pallas_call | solution.py:96
  868.5 24.0 %convert_bitcast_fusion.2.do_ref = bf16[1024,2048]{1,0:T(8,128)(2,1)} fusion(bf16[1024,4096]{1,0:T(8,128)(2,1)} %collective-permute-done.10, bf16[4096,4096]{1,0:T(8,128)(2,1)} %param.18, s32[]{:T(128)S(6)} %select_n.131), kind=kOutput, calls=%fused_computation.80 | convolution fusion | flops 17181966336 | bytes 29360132 | tf_op jit(solution)/shard_map/dot_general | solution.py:26
  892.4 49.4 %attn_bwd.7 = (bf16[1024,2048]{1,0:T(8,128)(2,1)}, f32[4096,256]{1,0:T(8,128)}, f32[4096,256]{1,0:T(8,128)}) custom-call(s32[4]{0:T(128)} %and_select_fusion.3.lo_ref, s32[4]{0:T(128)} %get-tuple-element.140.hi_ref, s32[4]{0:T(128)} %get-tuple-element.141.t0_ref, bf16[1024,2048]{1,0:T(8,128)(2,1)} %copy.129.q_ref, ...), custom_call_target="tpu_custom_call" | custom-call | flops 21474836480 | bytes 16777216 | tf_op jit(solution)/shard_map/attn_bwd/pallas_call | solution.py:175
  941.9 4.6 constant_dynamic-update-slice_fusion.3
  948.8 6.4 collective-permute-start.11
  955.2 43.9 %add_convert_fusion.1 = bf16[4096,2048]{0,1:T(8,128)(2,1)} fusion(f32[4096,2048]{0,1:T(8,128)} %fusion.122, f32[4096,2048]{0,1:T(8,128)} %fusion.120, f32[4096,2048]{0,1:T(8,128)} %fusion.121, bf16[1024,4096]{1,0:T(8,128)(2,1)} %collective-permute-done.8, bf16[1024,2048]{1,0:T(8,128)(2,1)} %get-tuple-element.47), kind=kOutput, calls=%fused_computation.3 | convolution fusion | flops 17213423616 | bytes 130023424 | tf_op jit(solution)/shard_map/dot_general | solution.py:26
  999.2 43.3 %add_convert_fusion = bf16[2048,4096]{1,0:T(8,128)(2,1)} fusion(f32[2048,4096]{1,0:T(8,128)} %fusion.124, f32[2048,4096]{1,0:T(8,128)} %fusion.107, f32[2048,4096]{1,0:T(8,128)} %fusion.123, bf16[1024,2048]{1,0:T(8,128)(2,1)S(1)} %copy-done.7, bf16[1024,4096]{1,0:T(8,128)(2,1)} %collective-permute-done.10), kind=kOutput, calls=%fused_computation.2 | convolution fusion | flops 17213423616 | bytes 130023424 | tf_op jit(solution)/shard_map/dot_general | solution.py:26
  1042.9 7.3 add_convert_fusion.4
  1050.9 9.4 fusion.64
  1061.5 8.6 fusion.113
  1070.1 46.5 %fusion.9 = (f32[4096]{0:T(1024)S(1)}, f32[1024]{0:T(1024)S(1)}, bf16[1024,4096]{1,0:T(8,128)(2,1)}) fusion(bf16[1,1024,4096]{2,1,0:T(8,128)(2,1)} %param.10, f32[1024]{0:T(1024)S(1)} %copy-done.26, f32[4096]{0:T(1024)S(1)} %copy-done.22, f32[1024,4096]{1,0:T(8,128)} %fusion.113, bf16[4096,4096]{1,0:T(8,128)(2,1)} %param.15, ...), kind=kOutput, calls=%fused_computation.20 | convolution fusion | flops 34418454528 | bytes 75538432 | tf_op jit(solution)/shard_map/dot_general | solution.py:26
  1116.6 13.9 %convert_reduce_fusion = (f32[4096]{0:T(1024)S(1)}, bf16[1,1024,4096]{2,1,0:T(8,128)(2,1)}) fusion(bf16[1,1024,4096]{2,1,0:T(8,128)(2,1)} %param.13, f32[1024]{0:T(1024)S(1)} %multiply_multiply_fusion, bf16[1,1024,4096]{2,1,0:T(8,128)(2,1)} %param.10, f32[1024]{0:T(1024)S(1)} %copy-done.26, f32[4096]{0:T(1024)S(1)} %copy-done.22, ...), kind=kLoop, calls=%fused_computation.14 | loop fusion | flops 46133248 | bytes 33595392 | tf_op jit(solution)/shard_map/reduce_sum | solution.py:293
  1130.5 10.5 psum.7
  1141.7 11.5 fusion.111
  1153.3 10.7 fusion.74
  1164.0 10.7 fusion.77
  1174.7 16.4 %add_convert_fusion.3 = bf16[4096,512]{1,0:T(8,128)(2,1)S(1)} fusion(f32[4096,512]{1,0:T(8,128)} %fusion.77, f32[4096,512]{1,0:T(8,128)} %fusion.111, f32[4096,512]{1,0:T(8,128)} %fusion.74, bf16[1024,4096]{1,0:T(8,128)(2,1)} %collective-permute-done.8, s32[]{:T(128)S(6)} %select_n.134, bf16[4096,256]{1,0:T(8,128)(2,1)} %copy-done, ...), kind=kOutput, calls=%fused_computation.67 | convolution fusion | flops 4305453056 | bytes 41943044 | tf_op jit(solution)/shard_map/dot_general | solution.py:26
  1193.4 22.5 %broadcast_select_fusion.3 = (bf16[4096,2048]{0,1:T(8,128)(2,1)}, bf16[4096,2048]{0,1:T(8,128)(2,1)}) fusion(bf16[4096,2048]{0,1:T(8,128)(2,1)} %add_convert_fusion.1, bf16[4096,2048]{0,1:T(8,128)(2,1)} %collective-permute-done.12, pred[]{:T(512)S(6)} %eq.4), kind=kLoop, calls=%fused_computation.31 | loop fusion | flops 16777216 | bytes 67108864 | tf_op jit(solution)/shard_map/jit(_where)/select_n | solution.py:207
  1215.9 23.8 %pad_maximum_fusion = bf16[4096,4096]{0,1:T(8,128)(2,1)} fusion(bf16[4096,2048]{0,1:T(8,128)(2,1)} %get-tuple-element.87, bf16[4096,2048]{0,1:T(8,128)(2,1)} %get-tuple-element.86), kind=kLoop, calls=%fused_computation | loop fusion | flops 67108864 | bytes 67108864 | tf_op jit(solution)/shard_map/concatenate | solution.py:209
  1239.7 44.1 %copy.118 = bf16[4096,4096]{1,0:T(8,128)(2,1)} copy(bf16[4096,4096]{0,1:T(8,128)(2,1)} %pad_maximum_fusion) | data formatting | bytes 67108864
  1283.8 22.5 %broadcast_select_fusion.1 = (bf16[2048,4096]{1,0:T(8,128)(2,1)}, bf16[2048,4096]{1,0:T(8,128)(2,1)}) fusion(bf16[2048,4096]{1,0:T(8,128)(2,1)} %add_convert_fusion, bf16[2048,4096]{1,0:T(8,128)(2,1)} %collective-permute-done.13, pred[]{:T(512)S(6)} %eq.4), kind=kLoop, calls=%fused_computation.29 | loop fusion | flops 16777216 | bytes 67108864 | tf_op jit(solution)/shard_map/jit(_where)/select_n | solution.py:207
  1306.3 23.8 %pad_maximum_fusion.1 = bf16[4096,4096]{1,0:T(8,128)(2,1)} fusion(bf16[2048,4096]{1,0:T(8,128)(2,1)} %get-tuple-element.85, bf16[2048,4096]{1,0:T(8,128)(2,1)} %get-tuple-element.84), kind=kLoop, calls=%fused_computation.1 | loop fusion | flops 67108864 | bytes 67108864 | tf_op jit(solution)/shard_map/concatenate | solution.py:209
  (169 shorter events, 39.8 us)
Async XLA Ops:
  0.6 5.3 copy-start.32
  0.7 5.3 copy-start.11
  0.7 5.8 copy-start.12
  0.7 35.4 %copy-start.36 = (f32[64]{0:T(128)}, f32[64]{0:T(128)S(1)}, u32[]{:S(2)}) copy-start(f32[64]{0:T(128)S(1)} %negate_power_fusion) | copy-start | bytes 772
  5.9 0.6 copy-start.23
  6.0 104.3 %copy-start.25 = (f32[1024]{0:T(1024)}, f32[1024]{0:T(1024)S(1)}, u32[]{:S(2)}) copy-start(f32[1024]{0:T(1024)S(1)} %fusion.93) | copy-start | bytes 12292
  6.0 104.3 %copy-start.21 = (f32[4096]{0:T(1024)}, f32[4096]{0:T(1024)S(1)}, u32[]{:S(2)}) copy-start(f32[4096]{0:T(1024)S(1)} %convert_add_fusion.1) | copy-start | bytes 49156
  6.7 11.9 copy-start.3
  18.6 7.2 copy-start.34
  18.6 7.2 copy-start.35
  36.1 4.9 copy-start.19
  41.0 92.0 %copy-start.9 = (f32[1024,64]{0,1:T(8,128)}, f32[1024,64]{0,1:T(8,128)S(1)}, u32[]{:S(2)}) copy-start(f32[1024,64]{0,1:T(8,128)S(1)} %get-tuple-element.122) | copy-start | bytes 786436
  41.0 92.0 %copy-start.10 = (f32[1024,64]{0,1:T(8,128)}, f32[1024,64]{0,1:T(8,128)S(1)}, u32[]{:S(2)}) copy-start(f32[1024,64]{0,1:T(8,128)S(1)} %get-tuple-element.136) | copy-start | bytes 786436
  45.8 101.1 %collective-permute-start = (bf16[1024,512]{1,0:T(8,128)(2,1)}, bf16[1024,512]{1,0:T(8,128)(2,1)S(1)}, u32[]{:S(2)}, u32[]{:S(2)}) collective-permute-start(bf16[1024,512]{1,0:T(8,128)(2,1)} %get-tuple-element.123), channel_id=1, source_target_pairs={{0,1},{1,0},{2,3},{3,2},{4,5},{5,4},{6,7},{7,6}} | collective-permute-start | bytes 3145736 | tf_op jit(solution)/shard_map/ppermute | solution.py:204
  45.8 98.6 %collective-permute-start.1 = (bf16[1024,512]{1,0:T(8,128)(2,1)}, bf16[1024,512]{1,0:T(8,128)(2,1)S(1)}, u32[]{:S(2)}, u32[]{:S(2)}) collective-permute-start(bf16[1024,512]{1,0:T(8,128)(2,1)} %get-tuple-element.123), channel_id=1, source_target_pairs={{0,2},{1,3},{2,0},{3,1},{4,6},{5,7},{6,4},{7,5}} | collective-permute-start | bytes 3145736 | tf_op jit(solution)/shard_map/ppermute | solution.py:201
  45.8 235.9 %collective-permute-start.7 = (bf16[1024,4096]{1,0:T(8,128)(2,1)}, bf16[1024,4096]{1,0:T(8,128)(2,1)}, u32[]{:S(2)}, u32[]{:S(2)}) collective-permute-start(bf16[1024,4096]{1,0:T(8,128)(2,1)} %fusion.7), channel_id=1, source_target_pairs={{0,2},{1,3},{2,0},{3,1},{4,6},{5,7},{6,4},{7,5}} | collective-permute-start | bytes 25165832 | tf_op jit(solution)/shard_map/ppermute | solution.py:201
  47.8 260.8 %collective-permute-start.3 = (bf16[1024,4096]{1,0:T(8,128)(2,1)}, bf16[1024,4096]{1,0:T(8,128)(2,1)}, u32[]{:S(2)}, u32[]{:S(2)}) collective-permute-start(bf16[1024,4096]{1,0:T(8,128)(2,1)} %fusion.7), channel_id=1, source_target_pairs={{0,1},{1,0},{2,3},{3,2},{4,5},{5,4},{6,7},{7,6}} | collective-permute-start | bytes 25165832 | tf_op jit(solution)/shard_map/ppermute | solution.py:204
  47.8 530.1 %collective-permute-start.9 = (bf16[1024,4096]{1,0:T(8,128)(2,1)}, bf16[1024,4096]{1,0:T(8,128)(2,1)}, u32[]{:S(2)}, u32[]{:S(2)}) collective-permute-start(bf16[1024,4096]{1,0:T(8,128)(2,1)} %bitcast.164), channel_id=1, source_target_pairs={{0,2},{1,3},{2,0},{3,1},{4,6},{5,7},{6,4},{7,5}} | collective-permute-start | bytes 25165832 | tf_op jit(solution)/shard_map/ppermute | solution.py:201
  50.0 24.9 %copy-start.27 = (s32[1024]{0:T(1024)}, s32[1024]{0:T(1024)S(1)}, u32[]{:S(2)}) copy-start(s32[1024]{0:T(1024)S(1)} %get-tuple-element.128) | copy-start | bytes 12292
  50.0 24.9 %copy-start.28 = (s32[1024]{0:T(1024)}, s32[1024]{0:T(1024)S(1)}, u32[]{:S(2)}) copy-start(s32[1024]{0:T(1024)S(1)} %get-tuple-element.127) | copy-start | bytes 12292
  50.0 24.9 %copy-start.29 = (s32[1024]{0:T(1024)}, s32[1024]{0:T(1024)S(1)}, u32[]{:S(2)}) copy-start(s32[1024]{0:T(1024)S(1)} %get-tuple-element.129) | copy-start | bytes 12292
  50.1 24.9 %copy-start.30 = (s32[1024]{0:T(1024)}, s32[1024]{0:T(1024)S(1)}, u32[]{:S(2)}) copy-start(s32[1024]{0:T(1024)S(1)} %get-tuple-element.130) | copy-start | bytes 12292
  133.6 3.2 copy-start.33
  144.4 4.8 collective-permute-start.2
  146.8 295.1 %collective-permute-start.5 = (bf16[1024,4096]{1,0:T(8,128)(2,1)}, bf16[1024,4096]{1,0:T(8,128)(2,1)}, u32[]{:S(2)}, u32[]{:S(2)}) collective-permute-start(bf16[1024,4096]{1,0:T(8,128)(2,1)} %bitcast.165), channel_id=1, source_target_pairs={{0,1},{1,0},{2,3},{3,2},{4,5},{5,4},{6,7},{7,6}} | collective-permute-start | bytes 25165832 | tf_op jit(solution)/shard_map/ppermute | solution.py:204
  308.6 24.5 %copy-start.15 = (f32[1024,64]{0,1:T(8,128)S(1)}, f32[1024,64]{0,1:T(8,128)}, u32[]{:S(2)}) copy-start(f32[1024,64]{0,1:T(8,128)} %get-tuple-element.119) | copy-start | bytes 786436
  308.6 24.5 %copy-start.16 = (f32[1024,64]{0,1:T(8,128)S(1)}, f32[1024,64]{0,1:T(8,128)}, u32[]{:S(2)}) copy-start(f32[1024,64]{0,1:T(8,128)} %get-tuple-element.139) | copy-start | bytes 786436
  338.6 9.0 copy-start.17
  338.6 9.0 copy-start.18
  408.0 348.5 %collective-permute-start.4 = (bf16[1024,2048]{1,0:T(8,128)(2,1)}, bf16[1024,2048]{1,0:T(8,128)(2,1)}, u32[]{:S(2)}, u32[]{:S(2)}) collective-permute-start(bf16[1024,2048]{1,0:T(8,128)(2,1)} %get-tuple-element.29.o_ref), channel_id=1, source_target_pairs={{0,1},{1,0},{2,3},{3,2},{4,5},{5,4},{6,7},{7,6}} | collective-permute-start | bytes 12582920 | tf_op jit(solution)/shard_map/ppermute | solution.py:204
  540.8 258.0 %collective-permute-start.6 = (bf16[1024,2048]{1,0:T(8,128)(2,1)}, bf16[1024,2048]{1,0:T(8,128)(2,1)}, u32[]{:S(2)}, u32[]{:S(2)}) collective-permute-start(bf16[1024,2048]{1,0:T(8,128)(2,1)} %get-tuple-element.35), channel_id=1, source_target_pairs={{0,1},{1,0},{2,3},{3,2},{4,5},{5,4},{6,7},{7,6}} | collective-permute-start | bytes 12582920 | tf_op jit(solution)/shard_map/ppermute | solution.py:204
  540.8 263.2 %collective-permute-start.8 = (bf16[1024,4096]{1,0:T(8,128)(2,1)}, bf16[1024,4096]{1,0:T(8,128)(2,1)}, u32[]{:S(2)}, u32[]{:S(2)}) collective-permute-start(bf16[1024,4096]{1,0:T(8,128)(2,1)} %collective-permute-done.7), channel_id=1, source_target_pairs={{0,1},{1,0},{2,3},{3,2},{4,5},{5,4},{6,7},{7,6}} | collective-permute-start | bytes 25165832 | tf_op jit(solution)/shard_map/ppermute | solution.py:204
  577.9 24.1 %copy-start.39 = (bf16[1024,2048]{1,0:T(8,128)(2,1)S(1)}, bf16[1024,2048]{1,0:T(8,128)(2,1)}, u32[]{:S(2)}) copy-start(bf16[1024,2048]{1,0:T(8,128)(2,1)} %get-tuple-element.35) | copy-start | bytes 12582916
  601.9 23.4 %copy-start.38 = (bf16[1024,2048]{1,0:T(8,128)(2,1)S(1)}, bf16[1024,2048]{1,0:T(8,128)(2,1)}, u32[]{:S(2)}) copy-start(bf16[1024,2048]{1,0:T(8,128)(2,1)} %get-tuple-element.29.o_ref) | copy-start | bytes 12582916
  601.9 266.5 %collective-permute-start.10 = (bf16[1024,4096]{1,0:T(8,128)(2,1)}, bf16[1024,4096]{1,0:T(8,128)(2,1)}, u32[]{:S(2)}, u32[]{:S(2)}) collective-permute-start(bf16[1024,4096]{1,0:T(8,128)(2,1)} %collective-permute-done.9), channel_id=1, source_target_pairs={{0,1},{1,0},{2,3},{3,2},{4,5},{5,4},{6,7},{7,6}} | collective-permute-start | bytes 25165832 | tf_op jit(solution)/shard_map/ppermute | solution.py:204
  625.3 23.8 %copy-start.40 = (bf16[1024,2048]{1,0:T(8,128)(2,1)S(1)}, bf16[1024,2048]{1,0:T(8,128)(2,1)}, u32[]{:S(2)}) copy-start(bf16[1024,2048]{1,0:T(8,128)(2,1)} %get-tuple-element.38.o_ref) | copy-start | bytes 12582916
  730.3 26.2 %copy-start.6 = (bf16[1024,2048]{1,0:T(8,128)(2,1)S(1)}, bf16[1024,2048]{1,0:T(8,128)(2,1)}, u32[]{:S(2)}) copy-start(bf16[1024,2048]{1,0:T(8,128)(2,1)} %get-tuple-element.28.o_ref) | copy-start | bytes 12582916
  756.5 2.5 copy-start.31
  759.1 39.7 %copy-start.5 = (bf16[1024,2048]{1,0:T(8,128)(2,1)S(1)}, bf16[1024,2048]{1,0:T(8,128)(2,1)}, u32[]{:S(2)}) copy-start(bf16[1024,2048]{1,0:T(8,128)(2,1)} %get-tuple-element.31) | copy-start | bytes 12582916
  827.2 1.0 copy-start.13
  827.2 1.0 copy-start.14
  941.9 4.6 copy-start.8
  948.8 94.1 %collective-permute-start.11 = (f32[4096,512]{1,0:T(8,128)}, f32[4096,512]{1,0:T(8,128)}, u32[]{:S(2)}, u32[]{:S(2)}) collective-permute-start(f32[4096,512]{1,0:T(8,128)} %constant_dynamic-update-slice_fusion.2), channel_id=1, source_target_pairs={{0,1},{1,0},{2,3},{3,2},{4,5},{5,4},{6,7},{7,6}} | collective-permute-start | bytes 25165832 | tf_op jit(solution)/shard_map/ppermute | solution.py:204
  955.2 44.0 %copy-start.7 = (bf16[1024,2048]{1,0:T(8,128)(2,1)S(1)}, bf16[1024,2048]{1,0:T(8,128)(2,1)}, u32[]{:S(2)}) copy-start(bf16[1024,2048]{1,0:T(8,128)(2,1)} %get-tuple-element.36.o_ref) | copy-start | bytes 12582916
  999.1 194.2 %collective-permute-start.12 = (bf16[4096,2048]{0,1:T(8,128)(2,1)}, bf16[4096,2048]{0,1:T(8,128)(2,1)}, u32[]{:S(2)}, u32[]{:S(2)}) collective-permute-start(bf16[4096,2048]{0,1:T(8,128)(2,1)} %add_convert_fusion.1), channel_id=1, source_target_pairs={{0,1},{1,0},{2,3},{3,2},{4,5},{5,4},{6,7},{7,6}} | collective-permute-start | bytes 50331656 | tf_op jit(solution)/shard_map/ppermute | solution.py:204
  1042.4 241.4 %collective-permute-start.13 = (bf16[2048,4096]{1,0:T(8,128)(2,1)}, bf16[2048,4096]{1,0:T(8,128)(2,1)}, u32[]{:S(2)}, u32[]{:S(2)}) collective-permute-start(bf16[2048,4096]{1,0:T(8,128)(2,1)} %add_convert_fusion), channel_id=1, source_target_pairs={{0,1},{1,0},{2,3},{3,2},{4,5},{5,4},{6,7},{7,6}} | collective-permute-start | bytes 50331656 | tf_op jit(solution)/shard_map/ppermute | solution.py:204
  1050.2 0.7 copy-start.20
  1050.2 0.7 copy-start.37
  1050.7 19.3 %copy-start.1 = (bf16[4096,256]{1,0:T(8,128)(2,1)}, bf16[4096,256]{1,0:T(8,128)(2,1)S(1)}, u32[]{:S(2)}) copy-start(bf16[4096,256]{1,0:T(8,128)(2,1)S(1)} %get-tuple-element.106) | copy-start | bytes 6291460
  1050.8 10.7 copy-start.4
  1061.5 102.5 %copy-start = (bf16[4096,256]{1,0:T(8,128)(2,1)}, bf16[4096,256]{1,0:T(8,128)(2,1)S(1)}, u32[]{:S(2)}) copy-start(bf16[4096,256]{1,0:T(8,128)(2,1)S(1)} %maximum_bitcast_fusion) | copy-start | bytes 6291460
  1061.5 8.6 copy-start.22
  1061.5 8.6 copy-start.26
  1070.1 46.5 %copy-start.24 = (f32[1024]{0:T(1024)S(1)}, f32[1024]{0:T(1024)}, u32[]{:S(2)}) copy-start(f32[1024]{0:T(1024)} %copy-done.23) | copy-start | bytes 12292
  1141.7 11.5 copy-start.2

commit v2 on v1

v2 whole, which is shorter than its diff:
```python
import functools

import jax
import jax.numpy as jnp
from jax import lax
from jax.experimental import pallas as pl
from jax.experimental.pallas import tpu as pltpu
from jax.sharding import PartitionSpec as P


WINDOW = 2048
NORM_EPS = 1e-6
ROPE_BASE = 10000.0
NEG_BIG = -1e30
POS_BIG = 3e38
HEAD_DIM = 256
ROT_HALF = HEAD_DIM // 4

FWD_BQ, FWD_BK = 256, 512
BWD_BQ, BWD_BK = 512, 512
VMEM_LIMIT = 67043328

NT = (((1,), (1,)), ((), ()))
NN = (((1,), (0,)), ((), ()))
TN = (((0,), (0,)), ((), ()))


def dot(a, b, dims):
    return lax.dot_general(a, b, dims, preferred_element_type=jnp.float32)


def rms_norm(x_f32, gain_f32):
    mean_sq = jnp.mean(x_f32 * x_f32, axis=-1, keepdims=True)
    return (x_f32 * lax.rsqrt(mean_sq + NORM_EPS) * (1.0 + gain_f32)).astype(jnp.bfloat16)


def rope_tables(positions):
    rot_dim = 2 * ROT_HALF
    inv_freq = ROPE_BASE ** (-(jnp.arange(ROT_HALF, dtype=jnp.float32) * 2.0 / rot_dim))
    angles = positions.astype(jnp.float32)[:, None] * inv_freq
    return jnp.cos(angles), jnp.sin(angles)


def rotary(vals, cos_a, sin_a):
    a = vals[..., :ROT_HALF]
    b = vals[..., ROT_HALF:2 * ROT_HALF]
    cos_a, sin_a = cos_a[:, None, :], sin_a[:, None, :]
    return jnp.concatenate([a * cos_a - b * sin_a, b * cos_a + a * sin_a, vals[..., 2 * ROT_HALF:]], axis=-1)


def resident(shape):
    return pl.BlockSpec(shape, lambda *_: (0,) * len(shape), pipeline_mode=pl.Buffered(1))


def params(axes, **kwargs):
    return pltpu.CompilerParams(dimension_semantics=("arbitrary",) * axes, vmem_limit_bytes=VMEM_LIMIT, **kwargs)


def proj_kernel(dims, rope, core_ref, a0_ref, a1_ref, w_ref, *rest):
    out_ref = rest[-1]
    rows = a0_ref.shape[0]
    for piece, a_ref in enumerate((a0_ref, a1_ref)):
        y = dot(a_ref[...], w_ref[...], dims)
        r = slice(piece * rows, (piece + 1) * rows)
        if not rope:
            out_ref[r, :] = y.astype(jnp.bfloat16)
            continue
        cos_a, sin_a = rest[0][r, :], rest[1][r, :]
        for h in range(y.shape[1] // HEAD_DIM):
            c0, c1, c2 = h * HEAD_DIM, h * HEAD_DIM + 2 * ROT_HALF, (h + 1) * HEAD_DIM
            turned = y[:, c0:c1] * cos_a + pltpu.roll(y[:, c0:c1], ROT_HALF, 1) * sin_a
            out_ref[r, c0:c1] = (turned * HEAD_DIM ** -0.5).astype(jnp.bfloat16)
            out_ref[r, c1:c2] = (y[:, c1:c2] * HEAD_DIM ** -0.5).astype(jnp.bfloat16)


def proj_pair(a0, a1, w, core, by_rows, tables=()):
    rows, depth = a0.shape
    half = w.shape[0 if by_rows else 1] // 2
    bn = 512
    nb = half // bn
    if by_rows:
        w_spec = pl.BlockSpec((bn, depth), lambda j, c: (c[0] * nb + j, 0))
    else:
        w_spec = pl.BlockSpec((depth, bn), lambda j, c: (0, c[0] * nb + j))
    return pl.pallas_call(
        functools.partial(proj_kernel, NT if by_rows else NN, bool(tables)),
        grid_spec=pltpu.PrefetchScalarGridSpec(
            num_scalar_prefetch=1, grid=(nb,),
            in_specs=[resident(a0.shape), resident(a1.shape), w_spec] + [resident(t.shape) for t in tables],
            out_specs=pl.BlockSpec((2 * rows, bn), lambda j, c: (0, j))),
        out_shape=jax.ShapeDtypeStruct((2 * rows, half), jnp.bfloat16),
        compiler_params=params(1),
        cost_estimate=pl.CostEstimate(flops=4 * rows * depth * half, bytes_accessed=2 * (2 * rows * (depth + half) + depth * half), transcendentals=0),
        name="proj_pair",
    )(core, a0, a1, w, *tables)


def wgrad_kernel(pieces, whole, col_sum, carried, core_ref, *refs):
    a_refs, b_refs, outs = refs[:pieces], refs[pieces:2 * pieces], refs[2 * pieces:]
    if carried:
        outs[-1][...] = outs[0][...]
        outs = outs[2:-1]
    y = sum(dot(a[...], b[...], TN) for a, b in zip(a_refs, b_refs)).astype(jnp.bfloat16)
    outs[0][...] = y
    if whole:
        outs[1][...] = y
    if col_sum:
        @pl.when(pl.program_id(0) == 0)
        def _():
            outs[-1][...] = sum(jnp.sum(b[...].astype(jnp.float32), axis=0, keepdims=True) for b in b_refs)


def wgrad(a, b, core, rows, bm, bn, whole_axis=None, col_sum=False, carried=()):
    m, n = a[0][0].shape[1], b[0][0].shape[1]
    mb, nb = m // bm, n // bn
    out_specs = [pl.BlockSpec((bm, bn), lambda i, j, c: (i, j))]
    out_shape = [jax.ShapeDtypeStruct((m, n), jnp.bfloat16)]
    if whole_axis == 0:
        out_specs.append(pl.BlockSpec((bm, bn), lambda i, j, c: (c[0] * mb + i, j)))
        out_shape.append(jax.ShapeDtypeStruct((2 * m, n), jnp.bfloat16))
    if whole_axis == 1:
        out_specs.append(pl.BlockSpec((bm, bn), lambda i, j, c: (i, c[0] * nb + j)))
        out_shape.append(jax.ShapeDtypeStruct((m, 2 * n), jnp.bfloat16))
    if col_sum:
        out_specs.append(pl.BlockSpec((1, bn), lambda i, j, c: (0, jnp.where(i == 0, j, nb - 1))))
        out_shape.append(jax.ShapeDtypeStruct((1, n), jnp.float32))
    extra_specs, aliases = [], {}
    if carried:
        steps = mb * nb
        block = (carried[0].shape[0] // steps, carried[0].shape[1])
        extra_specs = [pl.BlockSpec(block, lambda i, j, c: (i * nb + j, 0)), pl.BlockSpec(memory_space=pl.ANY)]
        aliases = {2 + 2 * len(a): len(out_shape)}
        out_specs.append(pl.BlockSpec(block, lambda i, j, c: ((1 - c[0]) * steps + i * nb + j, 0)))
        out_shape.append(jax.ShapeDtypeStruct(carried[1].shape, carried[1].dtype))
    return pl.pallas_call(
        functools.partial(wgrad_kernel, len(a), whole_axis is not None, col_sum, bool(carried)),
        grid_spec=pltpu.PrefetchScalarGridSpec(
            num_scalar_prefetch=1, grid=(mb, nb),
            in_specs=[pl.BlockSpec((rows, bm), lambda i, j, c, r=r: (r, i)) for _, r in a]
            + [pl.BlockSpec((rows, bn), lambda i, j, c, r=r: (r, j)) for _, r in b] + extra_specs,
            out_specs=out_specs),
        out_shape=out_shape,
        input_output_aliases=aliases,
        compiler_params=params(2),
        cost_estimate=pl.CostEstimate(flops=2 * len(a) * rows * m * n, bytes_accessed=2 * (len(a) * rows * (m + n) + m * n), transcendentals=0),
        name="wgrad",
    )(core, *[val for val, _ in a], *[val for val, _ in b], *carried)


def place_kernel(core_ref, part_ref, whole_ref, out_ref):
    out_ref[...] = part_ref[...]


def place(part, whole, core, axis):
    bm, bn = 512, 2048
    m, n = part.shape
    if axis == 0:
        out_spec = pl.BlockSpec((bm, bn), lambda i, j, c: ((1 - c[0]) * (m // bm) + i, j))
    else:
        out_spec = pl.BlockSpec((bm, bn), lambda i, j, c: (i, (1 - c[0]) * (n // bn) + j))
    return pl.pallas_call(
        place_kernel,
        grid_spec=pltpu.PrefetchScalarGridSpec(
            num_scalar_prefetch=1, grid=(m // bm, n // bn),
            in_specs=[pl.BlockSpec((bm, bn), lambda i, j, c: (i, j)), pl.BlockSpec(memory_space=pl.ANY)],
            out_specs=out_spec),
        out_shape=jax.ShapeDtypeStruct(whole.shape, whole.dtype),
        input_output_aliases={2: 0},
        compiler_params=params(2),
        cost_estimate=pl.CostEstimate(flops=m * n, bytes_accessed=4 * m * n, transcendentals=0),
        name="place",
    )(core, part, whole)


def join_kernel(dims, extra, core_ref, mine_ref, theirs_ref, w_mine_ref, w_theirs_ref, *rest):
    y = dot(mine_ref[...], w_mine_ref[...], dims) + dot(theirs_ref[...], w_theirs_ref[...], dims)
    if extra:
        y = rest[0][...].astype(jnp.float32) + y + rest[1][...].astype(jnp.float32)
    rest[-1][...] = y.astype(rest[-1].dtype)


def join_heads(mine, theirs, w, core, by_rows, extra=()):
    rows, half = theirs.shape
    bn = 512
    n = w.shape[0 if by_rows else 1]
    act = pl.BlockSpec((rows, half), lambda j, c: (0, 0), pipeline_mode=pl.Buffered(1))
    if by_rows:
        w_specs = [pl.BlockSpec((bn, half), lambda j, c: (j, c[0])), pl.BlockSpec((bn, half), lambda j, c: (j, 1 - c[0]))]
    else:
        w_specs = [pl.BlockSpec((half, bn), lambda j, c: (c[0], j)), pl.BlockSpec((half, bn), lambda j, c: (1 - c[0], j))]
    out_spec = pl.BlockSpec((rows, bn), lambda j, c: (0, j))
    extra_specs = [out_spec, pl.BlockSpec((1, bn), lambda j, c: (0, j))] if extra else []
    return pl.pallas_call(
        functools.partial(join_kernel, NT if by_rows else NN, bool(extra)),
        grid_spec=pltpu.PrefetchScalarGridSpec(
            num_scalar_prefetch=1, grid=(n // bn,), in_specs=[act, act] + w_specs + extra_specs, out_specs=out_spec),
        out_shape=jax.ShapeDtypeStruct((rows, n), jnp.bfloat16 if extra else jnp.float32),
        compiler_params=params(1),
        cost_estimate=pl.CostEstimate(flops=4 * rows * half * n, bytes_accessed=4 * (rows * half + half * n + rows * n), transcendentals=0),
        name="join_heads",
    )(core, mine, theirs, w, w, *extra)


def finish_kernel(y_ref, x_ref, g_ref, gain_ref, dkv_ref, w_kv_ref, out_ref, gain_out_ref):
    d_normed = (y_ref[...] + dot(dkv_ref[...], w_kv_ref[...], NT)).astype(jnp.bfloat16).astype(jnp.float32)
    x_f32 = x_ref[...].astype(jnp.float32)
    scale = lax.rsqrt(jnp.mean(x_f32 * x_f32, axis=1, keepdims=True) + NORM_EPS)
    unit = x_f32 * scale
    d_unit = d_normed * (1.0 + gain_ref[...].astype(jnp.float32))
    dx = scale * (d_unit - unit * jnp.mean(d_unit * unit, axis=1, keepdims=True))
    out_ref[...] = (g_ref[...].astype(jnp.float32) + dx).astype(jnp.bfloat16)

    @pl.when(pl.program_id(0) == 0)
    def _():
        gain_out_ref[...] = jnp.zeros_like(gain_out_ref)

    gain_out_ref[...] += jnp.sum(d_normed * unit, axis=0, keepdims=True)


def finish(y, x, g, gain, dkv, w_kv):
    rows, dim = x.shape
    br = 128
    tile = pl.BlockSpec((br, dim), lambda i: (i, 0))
    line = pl.BlockSpec((1, dim), lambda i: (0, 0))
    return pl.pallas_call(
        finish_kernel,
        grid=(rows // br,),
        in_specs=[tile, tile, tile, line, pl.BlockSpec((br, dkv.shape[1]), lambda i: (i, 0)), resident(w_kv.shape)],
        out_specs=[tile, line],
        out_shape=[jax.ShapeDtypeStruct((rows, dim), jnp.bfloat16), jax.ShapeDtypeStruct((1, dim), jnp.float32)],
        compiler_params=params(1),
        cost_estimate=pl.CostEstimate(flops=2 * rows * dim * dkv.shape[1], bytes_accessed=10 * rows * dim, transcendentals=0),
        name="finish",
    )(y, x, g, gain[None], dkv, w_kv)


def key_cap(k0, first_key, own_key, bk, bq):
    key_idx = k0 + lax.broadcasted_iota(jnp.int32, (bk, bq), 0)
    return jnp.where((key_idx >= first_key) & (key_idx <= own_key), POS_BIG, NEG_BIG)


def block_bounds(first_key, token, bq, bk):
    starts = token.reshape(-1, bq)[:, 0]
    return first_key.reshape(-1, bq)[:, 0] // bk, (starts + bq - 1) // bk + 1, starts


def head_cols(h):
    return slice(h * HEAD_DIM, (h + 1) * HEAD_DIM)


def fwd_kernel(bq, bk, heads, lo_ref, hi_ref, t0_ref, q_ref, k_ref, vt_ref, first_ref, o_ref, lse_ref, m_s, l_s, acc_s):
    i = pl.program_id(0)
    first_key = first_ref[0]
    own_key = t0_ref[i] + lax.broadcasted_iota(jnp.int32, (1, bq), 1)
    m_s[...] = jnp.full_like(m_s, NEG_BIG)
    l_s[...] = jnp.zeros_like(l_s)
    acc_s[...] = jnp.zeros_like(acc_s)

    def body(j, carry):
        k0 = pl.multiple_of(j * bk, bk)
        k_blk = k_ref[pl.ds(k0, bk), :]
        vt_blk = vt_ref[:, pl.ds(k0, bk)]
        cap = key_cap(k0, first_key, own_key, bk, bq)

        def scores(h):
            return dot(k_blk, q_ref[:, head_cols(h)], NT)

        def soften(h, s):
            s = jnp.minimum(s, cap)
            m_old = m_s[h:h + 1]
            m_new = jnp.maximum(m_old, jnp.max(s, axis=0, keepdims=True))
            p = jnp.exp(s - m_new)
            alpha = jnp.exp(m_old - m_new)
            l_s[h:h + 1] = l_s[h:h + 1] * alpha + jnp.sum(p, axis=0, keepdims=True)
            m_s[h:h + 1] = m_new
            return p.astype(jnp.bfloat16), alpha

        def gather_values(h, p, alpha):
            acc_s[h] = acc_s[h] * alpha + dot(vt_blk, p, NN)

        s, held = scores(0), None
        for h in range(heads):
            s_next = scores(h + 1) if h + 1 < heads else None
            now = soften(h, s)
            if held is not None:
                gather_values(h - 1, *held)
            held, s = now, s_next
        gather_values(heads - 1, *held)
        return carry

    lax.fori_loop(lo_ref[i], hi_ref[i], body, 0)
    for h in range(heads):
        l_h = l_s[h:h + 1]
        o_ref[:, head_cols(h)] = (acc_s[h] / l_h).T.astype(jnp.bfloat16)
        lse_ref[0, h:h + 1] = m_s[h:h + 1] + jnp.log(l_h)


def attn_fwd(q, k, vt, first_key, token):
    bq, bk = FWD_BQ, FWD_BK
    tokens, width = q.shape
    heads, nq = width // HEAD_DIM, tokens // bq
    return pl.pallas_call(
        functools.partial(fwd_kernel, bq, bk, heads),
        grid_spec=pltpu.PrefetchScalarGridSpec(
            num_scalar_prefetch=3, grid=(nq,),
            in_specs=[pl.BlockSpec((bq, width), lambda i, *_: (i, 0)), resident(k.shape), resident(vt.shape),
                      pl.BlockSpec((1, 1, bq), lambda i, *_: (i, 0, 0))],
            out_specs=[pl.BlockSpec((bq, width), lambda i, *_: (i, 0)), pl.BlockSpec((1, heads, bq), lambda i, *_: (i, 0, 0))],
            scratch_shapes=[pltpu.VMEM((heads, bq), jnp.float32), pltpu.VMEM((heads, bq), jnp.float32),
                            pltpu.VMEM((heads, HEAD_DIM, bq), jnp.float32)]),
        out_shape=[jax.ShapeDtypeStruct(q.shape, jnp.bfloat16), jax.ShapeDtypeStruct((nq, heads, bq), jnp.float32)],
        compiler_params=params(1),
        cost_estimate=pl.CostEstimate(flops=4 * tokens * width * 2048, bytes_accessed=4 * tokens * width, transcendentals=0),
        name="attn_fwd",
    )(*block_bounds(first_key, token, bq, bk), q, k, vt, first_key.reshape(nq, 1, bq))


def bwd_kernel(bq, bk, heads, add_in, lo_ref, hi_ref, t0_ref, q_ref, do_ref, o_ref, lse_ref, first_ref, cos_ref, sin_ref,
               k_ref, kt_ref, v_ref, *rest):
    dq_ref, dk_ref, dv_ref, dq_s, delta_s = rest[-5:]
    i = pl.program_id(0)

    @pl.when(i == 0)
    def _():
        dk_ref[...] = rest[0][...] if add_in else jnp.zeros_like(dk_ref)
        dv_ref[...] = rest[1][...] if add_in else jnp.zeros_like(dv_ref)

    first_key = first_ref[0]
    own_key = t0_ref[i] + lax.broadcasted_iota(jnp.int32, (1, bq), 1)
    dq_s[...] = jnp.zeros_like(dq_s)
    for h in range(heads):
        row_dot = jnp.sum(do_ref[:, head_cols(h)].astype(jnp.float32) * o_ref[:, head_cols(h)].astype(jnp.float32), axis=1, keepdims=True)
        delta_s[h:h + 1] = jnp.broadcast_to(row_dot, (bq, 128)).T[0:1]

    def body(j, carry):
        k0 = pl.multiple_of(j * bk, bk)
        k_blk = k_ref[pl.ds(k0, bk), :]
        v_blk = v_ref[pl.ds(k0, bk), :]
        kt_blk = kt_ref[:, pl.ds(k0, bk)]
        cap = key_cap(k0, first_key, own_key, bk, bq)
        p_all, ds_all = [], []
        for h in range(heads):
            s = jnp.minimum(dot(k_blk, q_ref[:, head_cols(h)], NT), cap)
            p = jnp.exp(s - lse_ref[0, h:h + 1])
            dp = dot(v_blk, do_ref[:, head_cols(h)], NT)
            ds = (p * (dp - delta_s[h:h + 1])).astype(jnp.bfloat16)
            p_all.append(p.astype(jnp.bfloat16))
            ds_all.append(ds)
            dq_s[h] += dot(kt_blk, ds, NN)
        q_rows = jnp.concatenate([q_ref[:, head_cols(h)] for h in range(heads)], axis=0)
        do_rows = jnp.concatenate([do_ref[:, head_cols(h)] for h in range(heads)], axis=0)
        dv_ref[pl.ds(k0, bk), :] += dot(jnp.concatenate(p_all, axis=1), do_rows, NN)
        dk_ref[pl.ds(k0, bk), :] += dot(jnp.concatenate(ds_all, axis=1), q_rows, NN)
        return carry

    lax.fori_loop(lo_ref[i], hi_ref[i], body, 0)
    cos_t, sin_t = cos_ref[...], sin_ref[...]
    for h in range(heads):
        dq = dq_s[h].astype(jnp.bfloat16).astype(jnp.float32)
        a, b = dq[:ROT_HALF], dq[ROT_HALF:2 * ROT_HALF]
        dq_lin = jnp.concatenate([a * cos_t + b * sin_t, b * cos_t - a * sin_t, dq[2 * ROT_HALF:]], axis=0) * HEAD_DIM ** -0.5
        dq_ref[:, head_cols(h)] = dq_lin.T.astype(jnp.bfloat16)


def attn_bwd(q, d_o, o, lse, k, kt, v, first_key, token, cos_a, sin_a, sums):
    bq, bk = BWD_BQ, BWD_BK
    tokens, width = q.shape
    heads, nq = width // HEAD_DIM, tokens // bq
    lse = lse.transpose(1, 0, 2).reshape(heads, nq, bq).transpose(1, 0, 2)
    tile = pl.BlockSpec((bq, width), lambda i, *_: (i, 0))
    trig = pl.BlockSpec((ROT_HALF, bq), lambda i, *_: (0, i))
    whole_out = pl.BlockSpec(k.shape, lambda i, *_: (0, 0))
    acc_shape = jax.ShapeDtypeStruct(k.shape, jnp.float32)
    return pl.pallas_call(
        functools.partial(bwd_kernel, bq, bk, heads, bool(sums)),
        grid_spec=pltpu.PrefetchScalarGridSpec(
            num_scalar_prefetch=3, grid=(nq,),
            in_specs=[tile, tile, tile, pl.BlockSpec((1, heads, bq), lambda i, *_: (i, 0, 0)),
                      pl.BlockSpec((1, 1, bq), lambda i, *_: (i, 0, 0)), trig, trig]
            + [resident(val.shape) for val in (k, kt, v) + tuple(sums)],
            out_specs=[tile, whole_out, whole_out],
            scratch_shapes=[pltpu.VMEM((heads, HEAD_DIM, bq), jnp.float32), pltpu.VMEM((heads, bq), jnp.float32)]),
        out_shape=[jax.ShapeDtypeStruct(q.shape, jnp.bfloat16), acc_shape, acc_shape],
        compiler_params=params(1),
        cost_estimate=pl.CostEstimate(flops=10 * tokens * width * 2048, bytes_accessed=8 * tokens * width, transcendentals=0),
        name="attn_bwd",
    )(*block_bounds(first_key, token, bq, bk), q, d_o, o, lse, first_key.reshape(nq, 1, bq), cos_a.T, sin_a.T, k, kt, v, *sums)


def solution(mesh):
    row_spec = P("dp", "sp", None)
    tok_spec = P("dp", "sp")
    mat_spec = P(None, None)
    grad_mat = P("dp", None)
    chips_perm = [(0, 2), (1, 3), (2, 0), (3, 1)]
    cores_perm = [(0, 1), (1, 0), (2, 3), (3, 2)]

    def to_chip(val):
        return lax.ppermute(val, "sp", chips_perm)

    def to_core(val):
        return lax.ppermute(val, "sp", cores_perm)

    def local_step(x, seg_ids, positions, out_grad, norm_scale, w_q, w_k, w_v, w_o, b_o):
        x, out_grad = x[0], out_grad[0]
        chunk = x.shape[0]
        me = lax.axis_index("sp")
        core = me % 2
        core_arr = core.astype(jnp.int32).reshape(1)
        pieces = [me, me ^ 1, me ^ 2, me ^ 3]

        def ordered(mine, theirs, axis):
            first = jnp.where(core == 0, mine, theirs)
            second = jnp.where(core == 0, theirs, mine)
            return jnp.concatenate([first, second], axis=axis)

        def piece_rows(val, piece):
            return lax.dynamic_slice_in_dim(val, piece * chunk, chunk, axis=0)

        def pair_rows(val, pair):
            return jnp.concatenate([piece_rows(val, pieces[2 * pair]), piece_rows(val, pieces[2 * pair + 1])], axis=0)

        meta = lax.all_gather(jnp.stack([seg_ids[0], positions[0]]), "sp", axis=1, tiled=True)
        x, out_grad, meta = lax.optimization_barrier((x, out_grad, meta))
        seg_all, pos_all = meta[0], meta[1]
        seq = seg_all.shape[0]
        token = jnp.arange(seq, dtype=jnp.int32)
        is_start = jnp.concatenate([jnp.ones((1,), jnp.bool_), seg_all[1:] != seg_all[:-1]])
        doc_start = lax.cummax(jnp.where(is_start, token, 0))
        first_key = jnp.maximum(doc_start, token - (WINDOW - 1))
        cos_all, sin_all = rope_tables(pos_all)

        n_own = rms_norm(x.astype(jnp.float32), norm_scale.astype(jnp.float32))

        w_kv = jnp.concatenate([w_k, w_v], axis=1)
        kv_lin = dot(n_own, w_kv, NN)
        cos_own, sin_own = piece_rows(cos_all, me), piece_rows(sin_all, me)
        k_own = rotary(kv_lin[:, None, :HEAD_DIM], cos_own, sin_own)[:, 0].astype(jnp.bfloat16)
        kv_own = jnp.concatenate([k_own, kv_lin[:, HEAD_DIM:].astype(jnp.bfloat16)], axis=1)

        kv_2 = to_chip(kv_own)
        n_2 = to_chip(n_own)
        g_2 = to_chip(out_grad)
        n_1, kv_1, g_1 = to_core(n_own), to_core(kv_own), to_core(out_grad)
        kv_3, n_3, g_3 = to_core(kv_2), to_core(n_2), to_core(g_2)
        kv_all = jnp.zeros((seq, 2 * HEAD_DIM), jnp.bfloat16)
        for piece, val in zip(pieces, (kv_own, kv_1, kv_2, kv_3)):
            kv_all = lax.dynamic_update_slice_in_dim(kv_all, val, piece * chunk, axis=0)
        k_all, v_all = kv_all[:, :HEAD_DIM], kv_all[:, HEAD_DIM:]
        kt_all, vt_all = k_all.T, v_all.T

        n_all = [n_own, n_1, n_2, n_3]
        g_all = [out_grad, g_1, g_2, g_3]

        o_all, dq_all = [], []
        kv_sums = ()
        for pair in (0, 1):
            a, b = 2 * pair, 2 * pair + 1
            first_p, token_p = pair_rows(first_key, pair), pair_rows(token, pair)
            cos_p, sin_p = pair_rows(cos_all, pair), pair_rows(sin_all, pair)
            tables = (jnp.concatenate([cos_p, cos_p], axis=1), jnp.concatenate([-sin_p, sin_p], axis=1))
            q = proj_pair(n_all[a], n_all[b], w_q, core_arr, False, tables)
            o, lse = attn_fwd(q, k_all, vt_all, first_p, token_p)
            d_o = proj_pair(g_all[a], g_all[b], w_o, core_arr, True)
            dq, *kv_sums = attn_bwd(q, d_o, o, lse, k_all, kt_all, v_all, first_p, token_p, cos_p, sin_p, kv_sums)
            o_all.append(o)
            dq_all.append(dq)

        block_out = join_heads(o_all[0], to_core(o_all[0][chunk:]), w_o, core_arr, False, (x, b_o[None]))
        d_normed_q = join_heads(dq_all[0], to_core(dq_all[0][chunk:]), w_q, core_arr, True)

        dk, dv = kv_sums
        theirs = to_core(jnp.where(core == 0, dv, dk))
        mine = jnp.where(core == 0, dk, dv) + theirs
        turned = rotary(mine[:, None].astype(jnp.bfloat16).astype(jnp.float32), cos_all, -sin_all)[:, 0]
        mine_lin = jnp.where(core == 0, turned, mine).astype(jnp.bfloat16)
        mine_pieces = [piece_rows(mine_lin, piece) for piece in pieces]

        halves = [(0, 0), (0, 1), (1, 0), (1, 1)]
        w_o_part, w_o_grad, b_o_sum = wgrad([(o_all[i], r) for i, r in halves], [(g, 0) for g in g_all], core_arr, chunk, 512, 1024, 0, True)
        w_o_theirs = to_core(w_o_part)
        w_q_part, w_q_grad, w_o_grad = wgrad([(n, 0) for n in n_all], [(dq_all[i], r) for i, r in halves], core_arr, chunk, 512, 1024, 1,
                                             carried=(w_o_theirs, w_o_grad))
        w_q_theirs = to_core(w_q_part)
        mine_w, = wgrad([(n, 0) for n in n_all], [(val, 0) for val in mine_pieces], core_arr, chunk, 1024, HEAD_DIM)
        theirs_w = to_core(mine_w)
        w_k_grad = jnp.where(core == 0, mine_w, theirs_w)
        w_v_grad = jnp.where(core == 0, theirs_w, mine_w)

        dkv_tok = ordered(mine_pieces[0], to_core(mine_pieces[1]), 1)
        x_grad, gain_part = finish(d_normed_q, x, out_grad, norm_scale, dkv_tok, w_kv)
        w_q_grad = place(w_q_theirs, w_q_grad, core_arr, 1)
        gain_sum = gain_part[0] + to_core(gain_part[0])
        gain_sum = gain_sum + to_chip(gain_sum)
        return (block_out[None], x_grad[None], gain_sum.astype(jnp.bfloat16), w_q_grad, w_k_grad, w_v_grad, w_o_grad,
                b_o_sum[0].astype(jnp.bfloat16))

    return jax.shard_map(local_step, mesh=mesh,
                         in_specs=(row_spec, tok_spec, tok_spec, row_spec, P(None), mat_spec, mat_spec, mat_spec, mat_spec, P(None)),
                         out_specs=(row_spec, row_spec, P("dp"), grad_mat, grad_mat, grad_mat, grad_mat, P("dp")),
                         check_vma=False)
```

time: 1320 us -> 1350 us (1.023); the launches traced: 1330 us -> 1340 us
  matrix products: 577 us -> 8.36 us
  Pallas kernels: 363 us -> 851 us
  waiting for transfers between devices: 0.04 us -> 352 us
  other arithmetic: 178 us -> 68 us
  local copies, waits for them, and re-layouts: 145 us -> 46 us
  starting transfers between devices: 44.1 us -> 6.9 us
    dot_general x24 -> x1, matrix products: 577 us -> 8.36 us  [dot(): return lax.dot_general(a, b, dims, preferred_element_type=jnp.float32)]
    pallas_call x8 -> x15, Pallas kernels: 363 us -> 851 us  [the longest x2 222 us: attn_bwd(): pl.pallas_call(functools.partial(bwd_kernel, bq, bk, heads, bool(sums)),...]
    ppermute x3 -> x4, waiting for transfers between devices: 0.01 us -> 351 us  [to_chip(): return lax.ppermute(val, 'sp', chips_perm)]
    unnamed x85 -> x45, local copies, waits for them, and re-layouts: 50.2 us -> 6.09 us
    concatenate x2 -> x9, other arithmetic: 47.5 us -> 6.78 us  [the longest x4 2.39 us: pair_rows(): jnp.concatenate([piece_rows(val, pieces[2 * pair]), piece_rows(val, piece...]
    select_n x8, other arithmetic: 54.9 us -> 14.7 us  [the longest x1 4.68 us: local_step(): theirs = to_core(jnp.where(core == 0, dv, dk))]
    ppermute x11 -> x14, starting transfers between devices: 41.8 us -> 2.85 us  [to_core(): return lax.ppermute(val, 'sp', cores_perm)]
    dot_general x2 -> x0, local copies, waits for them, and re-layouts: 35.4 us -> none  [dot(): return lax.dot_general(a, b, dims, preferred_element_type=jnp.float32)]
  transfers between devices with their start and end apart: 14 -> 18, of which waited for: 0 -> 3; matrix products, arithmetic and copies ran while one was open for 59% -> 8% of each run, Pallas kernels for 24% -> 56%
where the time goes in v2:
time: 1350 us; the launch traced here: 1340 us
  Pallas kernels  851 us (63%)
  waiting for transfers between devices  352 us (26%)
  other arithmetic  68 us (5%)
  local copies, waits for them, and re-layouts  46 us (3%)
    ppermute x4, waiting for transfers between devices, to_chip(): return lax.ppermute(val, 'sp', chips_perm)  351 us
    pallas_call x2, Pallas kernels, attn_bwd(): pl.pallas_call(functools.partial(bwd_kernel, bq, bk, heads, bool(sums)),...  222 us
    pallas_call x3, Pallas kernels, wgrad(): pl.pallas_call(functools.partial(wgrad_kernel, len(a), whole_axis is not...  203 us
    pallas_call x4, Pallas kernels, proj_pair(): pl.pallas_call(functools.partial(proj_kernel, NT if by_rows else NN, bool...  177 us
    pallas_call x2, Pallas kernels, attn_fwd(): pl.pallas_call(functools.partial(fwd_kernel, bq, bk, heads), grid_spec=pl...  127 us
    pallas_call x2, Pallas kernels, join_heads(): pl.pallas_call(functools.partial(join_kernel, NT if by_rows else NN, bool...  85.3 us
  transfers between devices with their start and end apart: 18, of which 3 were waited for; matrix products, arithmetic and copies ran while one was open for 8% of the time, Pallas kernels for 56%

profile of v2, /device:TPU:0, one launch (start us, length us, event | category | flops | bytes accessed | tf_op | source)
XLA Modules:
  0.0 1344.0 jit_solution(6591394172383273576)
XLA Ops:
  0.6 0.7 pad_add_fusion
  1.4 10.0 all_gather.3
  11.3 5.1 fusion
  16.5 10.5 fusion.2.a0_ref.refs_0_
  27.0 2.0 collective-permute-start.9
  29.1 3.7 multiply_sine_fusion.1
  32.8 1.0 constant_dynamic-slice_fusion.5
  34.2 1.9 constant_dynamic-update-slice_fusion.1
  36.6 8.4 fusion.34
  45.7 2.3 broadcast_in_dim.36
  48.0 1.5 pad_maximum_fusion
  54.7 0.8 maximum_bitcast_fusion.1.cos_ref
  55.6 0.9 fusion.16
  57.8 0.9 fusion.18
  58.7 1.0 maximum_maximum_fusion.1
  59.7 350.0 %collective-permute-done.2 = bf16[1024,512]{1,0:T(8,128)(2,1)} collective-permute-done((bf16[1024,512]{1,0:T(8,128)(2,1)}, bf16[1024,512]{1,0:T(8,128)(2,1)}, u32[]{:S(2)}, u32[]{:S(2)}) %collective-permute-start.2) | collective-permute-done | bytes 1048608 | tf_op jit(solution)/shard_map/ppermute | solution.py:399
  410.3 1.1 maximum_maximum_fusion.2
  412.5 1.3 copy.65.rest_1_
  413.8 2.6 copy.64.rest_0_
  416.4 1.3 copy.57.rest_1_
  417.8 1.3 copy.56.rest_0_
  419.7 0.8 maximum_bitcast_fusion.3.cos_ref
  420.5 2.3 constant_dynamic-update-slice_fusion.4
  422.8 2.3 constant_dynamic-update-slice_fusion.3
  425.0 2.3 constant_dynamic-update-slice_fusion.2
  427.3 5.2 fusion.32
  432.5 4.1 copy.62.vt_ref
  436.5 2.8 copy.63.kt_ref
  439.9 44.5 %proj_pair.4.q_ref = bf16[2048,2048]{1,0:T(8,128)(2,1)} custom-call(s32[1]{0:T(128)} %bitcast.core_ref, bf16[1024,4096]{1,0:T(8,128)(2,1)} %fusion.2.a0_ref.refs_0_, bf16[1024,4096]{1,0:T(8,128)(2,1)} %collective-permute-done.a1_ref.refs_1_, bf16[4096,4096]{1,0:T(8,128)(2,1)} %w_ref.6, f32[2048,128]{1,0:T(8,128)} %copy.56.rest_0_, f32[2048,128]{1,0:T(8,128)} %copy.57.rest_1_), custom_call_target="tpu_custom_call" | custom-call | flops 34359738368 | bytes 41943040 | tf_op jit(solution)/shard_map/proj_pair/pallas_call | solution.py:85
  484.4 50.1 %attn_fwd.2 = (bf16[2048,2048]{1,0:T(8,128)(2,1)}, f32[8,8,256]{2,1,0:T(8,128)}) custom-call(s32[8]{0:T(128)} %get-tuple-element.91.lo_ref, s32[8]{0:T(128)} %get-tuple-element.92.hi_ref, s32[8]{0:T(128)} %copy-done.19, bf16[2048,2048]{1,0:T(8,128)(2,1)} %proj_pair.4.q_ref, bf16[4096,256]{1,0:T(8,128)(2,1)} %get-tuple-element.59.k_ref, ...), custom_call_target="tpu_custom_call" | custom-call | flops 34359738368 | bytes 16777216 | tf_op jit(solution)/shard_map/attn_fwd/pallas_call | solution.py:302
  534.5 43.9 %proj_pair.5.do_ref = bf16[2048,2048]{1,0:T(8,128)(2,1)} custom-call(s32[1]{0:T(128)} %bitcast.core_ref, bf16[1024,4096]{1,0:T(8,128)(2,1)} %bitcast.82, bf16[1024,4096]{1,0:T(8,128)(2,1)} %collective-permute-done.5.a1_ref.refs_5_, bf16[4096,4096]{1,0:T(8,128)(2,1)} %w_ref.7), custom_call_target="tpu_custom_call" | custom-call | flops 34359738368 | bytes 41943040 | tf_op jit(solution)/shard_map/proj_pair/pallas_call | solution.py:85
  578.4 44.9 %proj_pair.6.q_ref = bf16[2048,2048]{1,0:T(8,128)(2,1)} custom-call(s32[1]{0:T(128)} %bitcast.core_ref, bf16[1024,4096]{1,0:T(8,128)(2,1)} %collective-permute-done.7.a0_ref.refs_2_, bf16[1024,4096]{1,0:T(8,128)(2,1)} %collective-permute-done.8.a1_ref.refs_3_, bf16[4096,4096]{1,0:T(8,128)(2,1)} %w_ref.6, f32[2048,128]{1,0:T(8,128)} %copy.64.rest_0_, ...), custom_call_target="tpu_custom_call" | custom-call | flops 34359738368 | bytes 41943040 | tf_op jit(solution)/shard_map/proj_pair/pallas_call | solution.py:85
  623.3 76.6 %attn_fwd.3 = (bf16[2048,2048]{1,0:T(8,128)(2,1)}, f32[8,8,256]{2,1,0:T(8,128)}) custom-call(s32[8]{0:T(128)} %get-tuple-element.89.lo_ref, s32[8]{0:T(128)} %get-tuple-element.90.hi_ref, s32[8]{0:T(128)} %copy-done.18, bf16[2048,2048]{1,0:T(8,128)(2,1)} %proj_pair.6.q_ref, bf16[4096,256]{1,0:T(8,128)(2,1)} %get-tuple-element.59.k_ref, ...), custom_call_target="tpu_custom_call" | custom-call | flops 34359738368 | bytes 16777216 | tf_op jit(solution)/shard_map/attn_fwd/pallas_call | solution.py:302
  699.9 87.7 %wgrad.3 = (bf16[2048,4096]{1,0:T(8,128)(2,1)}, bf16[4096,4096]{1,0:T(8,128)(2,1)}, f32[1,4096]{1,0:T(1,128)}) custom-call(s32[1]{0:T(128)} %bitcast.core_ref, bf16[2048,2048]{1,0:T(8,128)(2,1)} %get-tuple-element.31.mine_ref.o_ref.refs_0_.refs_1_, bf16[2048,2048]{1,0:T(8,128)(2,1)} %get-tuple-element.31.mine_ref.o_ref.refs_0_.refs_1_, ...), custom_call_target="tpu_custom_call" | custom-call | flops 68719476736 | bytes 67108864 | tf_op jit(solution)/shard_map/wgrad/pallas_call | solution.py:135
  787.7 86.8 %attn_bwd.2 = (bf16[2048,2048]{1,0:T(8,128)(2,1)}, f32[4096,256]{1,0:T(8,128)}, f32[4096,256]{1,0:T(8,128)}) custom-call(s32[4]{0:T(128)} %and_select_fusion.5.lo_ref, s32[4]{0:T(128)} %fusion.30.hi_ref, s32[4]{0:T(128)} %copy-done.21, bf16[2048,2048]{1,0:T(8,128)(2,1)} %proj_pair.4.q_ref, bf16[2048,2048]{1,0:T(8,128)(2,1)} %proj_pair.5.do_ref, ...), custom_call_target="tpu_custom_call" | custom-call | flops 85899345920 | bytes 33554432 | tf_op jit(solution)/shard_map/attn_bwd/pallas_call | solution.py:374
  874.4 43.8 %proj_pair.7.do_ref = bf16[2048,2048]{1,0:T(8,128)(2,1)} custom-call(s32[1]{0:T(128)} %bitcast.core_ref, bf16[1024,4096]{1,0:T(8,128)(2,1)} %collective-permute-done.9.a0_ref.refs_6_, bf16[1024,4096]{1,0:T(8,128)(2,1)} %collective-permute-done.10.a1_ref.refs_7_, bf16[4096,4096]{1,0:T(8,128)(2,1)} %w_ref.7), custom_call_target="tpu_custom_call" | custom-call | flops 34359738368 | bytes 41943040 | tf_op jit(solution)/shard_map/proj_pair/pallas_call | solution.py:85
  918.2 135.1 %attn_bwd.3 = (bf16[2048,2048]{1,0:T(8,128)(2,1)}, f32[4096,256]{1,0:T(8,128)}, f32[4096,256]{1,0:T(8,128)}) custom-call(s32[4]{0:T(128)} %and_select_fusion.3.lo_ref, s32[4]{0:T(128)} %fusion.29.hi_ref, s32[4]{0:T(128)} %copy-done.20, bf16[2048,2048]{1,0:T(8,128)(2,1)} %proj_pair.6.q_ref, bf16[2048,2048]{1,0:T(8,128)(2,1)} %proj_pair.7.do_ref, ...), custom_call_target="tpu_custom_call" | custom-call | flops 85899345920 | bytes 33554432 | tf_op jit(solution)/shard_map/attn_bwd/pallas_call | solution.py:374
  1053.3 4.7 broadcast_select_fusion.2
  1058.5 98.2 %wgrad.4 = (bf16[4096,2048]{1,0:T(8,128)(2,1)}, bf16[4096,4096]{1,0:T(8,128)(2,1)}, bf16[4096,4096]{1,0:T(8,128)(2,1)}) custom-call(s32[1]{0:T(128)} %bitcast.core_ref, bf16[1024,4096]{1,0:T(8,128)(2,1)} %fusion.2.a0_ref.refs_0_, bf16[1024,4096]{1,0:T(8,128)(2,1)} %collective-permute-done.a1_ref.refs_1_, ...), custom_call_target="tpu_custom_call", output_to_operand_aliasing={{2}: (10, {})} | custom-call | flops 68719476736 | bytes 67108864 | tf_op jit(solution)/shard_map/wgrad/pallas_call | solution.py:135
  1156.8 5.1 slice.100
  1162.3 0.6 broadcast_in_dim.42.gain_ref
  1162.9 0.6 broadcast_in_dim.40.rest_1_
  1163.5 2.4 slice.97
  1166.0 1.2 copy-done
  1167.2 1.3 copy-done.1
  1168.5 3.0 bitcast_convert_fusion
  1171.7 9.1 fusion.7
  1180.7 3.8 fusion.4
  1184.5 1.3 copy-done.3
  1185.8 1.2 constant_dynamic-slice_fusion
  1187.0 1.2 collective-permute-done.6.theirs_ref
  1188.2 42.4 %join_heads.3.y_ref = f32[1024,4096]{1,0:T(8,128)} custom-call(s32[1]{0:T(128)} %bitcast.core_ref, bf16[2048,2048]{1,0:T(8,128)(2,1)} %get-tuple-element.34.mine_ref.refs_4_.refs_5_, bf16[1024,2048]{1,0:T(8,128)(2,1)} %collective-permute-done.6.theirs_ref, bf16[4096,4096]{1,0:T(8,128)(2,1)} %w_ref.6, bf16[4096,4096]{1,0:T(8,128)(2,1)} %w_ref.6), custom_call_target="tpu_custom_call" | custom-call | flops 34359738368 | bytes 58720256 | tf_op jit(solution)/shard_map/join_heads/pallas_call | solution.py:193
  1230.6 2.2 broadcast_select_fusion.4
  1232.8 16.8 %wgrad.5 = bf16[4096,256]{1,0:T(8,128)(2,1)} custom-call(s32[1]{0:T(128)} %bitcast.core_ref, bf16[1024,4096]{1,0:T(8,128)(2,1)} %fusion.2.a0_ref.refs_0_, bf16[1024,4096]{1,0:T(8,128)(2,1)} %collective-permute-done.a1_ref.refs_1_, bf16[1024,4096]{1,0:T(8,128)(2,1)} %collective-permute-done.7.a0_ref.refs_2_, ...), custom_call_target="tpu_custom_call" | custom-call | flops 8589934592 | bytes 37748736 | tf_op jit(solution)/shard_map/wgrad/pallas_call | solution.py:135
  1249.9 1.1 broadcast_select_fusion.3
  1251.0 2.1 pad_maximum_fusion.1.dkv_ref
  1253.1 24.0 %finish.1 = (bf16[1024,4096]{1,0:T(8,128)(2,1)}, f32[1,4096]{1,0:T(1,128)}) custom-call(f32[1024,4096]{1,0:T(8,128)} %join_heads.3.y_ref, bf16[1024,4096]{1,0:T(8,128)(2,1)} %bitcast.78, bf16[1024,4096]{1,0:T(8,128)(2,1)} %bitcast.84, bf16[1,4096]{1,0:T(2,128)(2,1)} %broadcast_in_dim.42.gain_ref, bf16[1024,512]{1,0:T(8,128)(2,1)} %pad_maximum_fusion.1.dkv_ref, ...), custom_call_target="tpu_custom_call" | custom-call | flops 4294967296 | bytes 41943040 | tf_op jit(solution)/shard_map/finish/pallas_call | solution.py:225
  1277.3 42.8 %join_heads.2 = bf16[1024,4096]{1,0:T(8,128)(2,1)} custom-call(s32[1]{0:T(128)} %bitcast.core_ref, bf16[2048,2048]{1,0:T(8,128)(2,1)} %get-tuple-element.31.mine_ref.o_ref.refs_0_.refs_1_, bf16[1024,2048]{1,0:T(8,128)(2,1)} %collective-permute-done.4.theirs_ref, bf16[4096,4096]{1,0:T(8,128)(2,1)} %w_ref.7, bf16[4096,4096]{1,0:T(8,128)(2,1)} %w_ref.7, ...), custom_call_target="tpu_custom_call" | custom-call | flops 34359738368 | bytes 58720256 | tf_op jit(solution)/shard_map/join_heads/pallas_call | solution.py:193
  1320.2 0.7 add.124
  1320.9 1.7 collective-permute-start.14
  1322.7 1.4 convert_reduce_fusion
  1324.0 0.6 collective-permute-done.14
  1325.3 4.5 broadcast_select_fusion
  1329.8 13.8 %place.1 = bf16[4096,4096]{1,0:T(8,128)(2,1)} custom-call(s32[1]{0:T(128)} %bitcast.core_ref, bf16[4096,2048]{1,0:T(8,128)(2,1)} %collective-permute-done.16.part_ref, bf16[4096,4096]{1,0:T(8,128)(2,1)} %get-tuple-element.47.whole_ref), custom_call_target="tpu_custom_call", output_to_operand_aliasing={{}: (2, {})} | custom-call | flops 8388608 | bytes 33554432 | tf_op jit(solution)/shard_map/place/pallas_call | solution.py:161
  (132 shorter events, 13.3 us)
Async XLA Ops:
  11.3 5.1 copy-start.13
  27.0 412.4 %collective-permute-start.7 = (bf16[1024,4096]{1,0:T(8,128)(2,1)}, bf16[1024,4096]{1,0:T(8,128)(2,1)}, u32[]{:S(2)}, u32[]{:S(2)}) collective-permute-start(bf16[1024,4096]{1,0:T(8,128)(2,1)} %fusion.2.a0_ref.refs_0_), channel_id=1, source_target_pairs={{0,2},{1,3},{2,0},{3,1},{4,6},{5,7},{6,4},{7,5}} | collective-permute-start | bytes 25165832 | tf_op jit(solution)/shard_map/ppermute | solution.py:399
  27.0 412.9 %collective-permute-start = (bf16[1024,4096]{1,0:T(8,128)(2,1)}, bf16[1024,4096]{1,0:T(8,128)(2,1)}, u32[]{:S(2)}, u32[]{:S(2)}) collective-permute-start(bf16[1024,4096]{1,0:T(8,128)(2,1)} %fusion.2.a0_ref.refs_0_), channel_id=1, source_target_pairs={{0,1},{1,0},{2,3},{3,2},{4,5},{5,4},{6,7},{7,6}} | collective-permute-start | bytes 25165832 | tf_op jit(solution)/shard_map/ppermute | solution.py:402
  27.0 412.4 %collective-permute-start.9 = (bf16[1024,4096]{1,0:T(8,128)(2,1)}, bf16[1024,4096]{1,0:T(8,128)(2,1)}, u32[]{:S(2)}, u32[]{:S(2)}) collective-permute-start(bf16[1024,4096]{1,0:T(8,128)(2,1)} %bitcast.80), channel_id=1, source_target_pairs={{0,2},{1,3},{2,0},{3,1},{4,6},{5,7},{6,4},{7,5}} | collective-permute-start | bytes 25165832 | tf_op jit(solution)/shard_map/ppermute | solution.py:399
  29.0 5.0 copy-start.16
  29.0 5.0 copy-start.11
  33.8 24.0 %copy-start.8 = (f32[1024,64]{0,1:T(8,128)}, f32[1024,64]{0,1:T(8,128)S(1)}, u32[]{:S(2)}) copy-start(f32[1024,64]{0,1:T(8,128)S(1)} %get-tuple-element.67) | copy-start | bytes 786436
  34.2 2.2 copy-start.10
  36.6 8.4 copy-start.2
  49.5 361.9 %collective-permute-start.1 = (bf16[1024,512]{1,0:T(8,128)(2,1)}, bf16[1024,512]{1,0:T(8,128)(2,1)}, u32[]{:S(2)}, u32[]{:S(2)}) collective-permute-start(bf16[1024,512]{1,0:T(8,128)(2,1)} %get-tuple-element.73), channel_id=1, source_target_pairs={{0,1},{1,0},{2,3},{3,2},{4,5},{5,4},{6,7},{7,6}} | collective-permute-start | bytes 3145736 | tf_op jit(solution)/shard_map/ppermute | solution.py:402
  49.7 360.0 %collective-permute-start.2 = (bf16[1024,512]{1,0:T(8,128)(2,1)}, bf16[1024,512]{1,0:T(8,128)(2,1)}, u32[]{:S(2)}, u32[]{:S(2)}) collective-permute-start(bf16[1024,512]{1,0:T(8,128)(2,1)} %get-tuple-element.73), channel_id=1, source_target_pairs={{0,2},{1,3},{2,0},{3,1},{4,6},{5,7},{6,4},{7,5}} | collective-permute-start | bytes 3145736 | tf_op jit(solution)/shard_map/ppermute | solution.py:399
  51.3 7.4 copy-start.18
  51.6 7.1 copy-start.19
  51.7 7.0 copy-start.21
  51.9 6.8 copy-start.20
  55.5 354.8 %copy-start.4 = (f32[1024,64]{0,1:T(8,128)S(1)}, f32[1024,64]{0,1:T(8,128)}, u32[]{:S(2)}) copy-start(f32[1024,64]{0,1:T(8,128)} %get-tuple-element.95) | copy-start | bytes 786436
  55.5 354.8 %copy-start.6 = (f32[1024,64]{0,1:T(8,128)S(1)}, f32[1024,64]{0,1:T(8,128)}, u32[]{:S(2)}) copy-start(f32[1024,64]{0,1:T(8,128)} %get-tuple-element.96) | copy-start | bytes 786436
  409.7 15.3 %collective-permute-start.3 = (bf16[1024,512]{1,0:T(8,128)(2,1)}, bf16[1024,512]{1,0:T(8,128)(2,1)}, u32[]{:S(2)}, u32[]{:S(2)}) collective-permute-start(bf16[1024,512]{1,0:T(8,128)(2,1)} %collective-permute-done.2), channel_id=1, source_target_pairs={{0,1},{1,0},{2,3},{3,2},{4,5},{5,4},{6,7},{7,6}} | collective-permute-start | bytes 3145736 | tf_op jit(solution)/shard_map/ppermute | solution.py:402
  411.4 123.1 %collective-permute-start.5 = (bf16[1024,4096]{1,0:T(8,128)(2,1)}, bf16[1024,4096]{1,0:T(8,128)(2,1)}, u32[]{:S(2)}, u32[]{:S(2)}) collective-permute-start(bf16[1024,4096]{1,0:T(8,128)(2,1)} %bitcast.81), channel_id=1, source_target_pairs={{0,1},{1,0},{2,3},{3,2},{4,5},{5,4},{6,7},{7,6}} | collective-permute-start | bytes 25165832 | tf_op jit(solution)/shard_map/ppermute | solution.py:402
  412.5 7.2 copy-start.5
  413.8 5.8 copy-start.7
  439.4 139.0 %collective-permute-start.8 = (bf16[1024,4096]{1,0:T(8,128)(2,1)}, bf16[1024,4096]{1,0:T(8,128)(2,1)}, u32[]{:S(2)}, u32[]{:S(2)}) collective-permute-start(bf16[1024,4096]{1,0:T(8,128)(2,1)} %collective-permute-done.7.a0_ref.refs_2_), channel_id=1, source_target_pairs={{0,1},{1,0},{2,3},{3,2},{4,5},{5,4},{6,7},{7,6}} | collective-permute-start | bytes 25165832 | tf_op jit(solution)/shard_map/ppermute | solution.py:402
  439.4 260.5 %collective-permute-start.10 = (bf16[1024,4096]{1,0:T(8,128)(2,1)}, bf16[1024,4096]{1,0:T(8,128)(2,1)}, u32[]{:S(2)}, u32[]{:S(2)}) collective-permute-start(bf16[1024,4096]{1,0:T(8,128)(2,1)} %collective-permute-done.9.a0_ref.refs_6_), channel_id=1, source_target_pairs={{0,1},{1,0},{2,3},{3,2},{4,5},{5,4},{6,7},{7,6}} | collective-permute-start | bytes 25165832 | tf_op jit(solution)/shard_map/ppermute | solution.py:402
  787.6 270.9 %collective-permute-start.15 = (bf16[2048,4096]{1,0:T(8,128)(2,1)}, bf16[2048,4096]{1,0:T(8,128)(2,1)}, u32[]{:S(2)}, u32[]{:S(2)}) collective-permute-start(bf16[2048,4096]{1,0:T(8,128)(2,1)} %get-tuple-element.44), channel_id=1, source_target_pairs={{0,1},{1,0},{2,3},{3,2},{4,5},{5,4},{6,7},{7,6}} | collective-permute-start | bytes 50331656 | tf_op jit(solution)/shard_map/ppermute | solution.py:402
  1058.0 108.0 %collective-permute-start.11 = (f32[4096,256]{1,0:T(8,128)}, f32[4096,256]{1,0:T(8,128)}, u32[]{:S(2)}, u32[]{:S(2)}) collective-permute-start(f32[4096,256]{1,0:T(8,128)} %broadcast_select_fusion.2), channel_id=1, source_target_pairs={{0,1},{1,0},{2,3},{3,2},{4,5},{5,4},{6,7},{7,6}} | collective-permute-start | bytes 12582920 | tf_op jit(solution)/shard_map/ppermute | solution.py:402
  1156.7 5.6 copy-start.14
  1156.7 6.2 copy-start.15
  1156.7 6.8 copy-start.9
  1156.7 173.1 %collective-permute-start.16 = (bf16[4096,2048]{1,0:T(8,128)(2,1)}, bf16[4096,2048]{1,0:T(8,128)(2,1)}, u32[]{:S(2)}, u32[]{:S(2)}) collective-permute-start(bf16[4096,2048]{1,0:T(8,128)(2,1)} %get-tuple-element.46), channel_id=1, source_target_pairs={{0,1},{1,0},{2,3},{3,2},{4,5},{5,4},{6,7},{7,6}} | collective-permute-start | bytes 50331656 | tf_op jit(solution)/shard_map/ppermute | solution.py:402
  1161.8 26.4 %collective-permute-start.6 = (bf16[1024,2048]{1,0:T(8,128)(2,1)}, bf16[1024,2048]{1,0:T(8,128)(2,1)}, u32[]{:S(2)}, u32[]{:S(2)}) collective-permute-start(bf16[1024,2048]{1,0:T(8,128)(2,1)} %slice.100), channel_id=1, source_target_pairs={{0,1},{1,0},{2,3},{3,2},{4,5},{5,4},{6,7},{7,6}} | collective-permute-start | bytes 12582920 | tf_op jit(solution)/shard_map/ppermute | solution.py:402
  1163.5 3.7 copy-start
  1163.5 5.0 copy-start.1
  1166.0 5.7 copy-start.12
  1166.0 5.7 copy-start.17
  1166.0 111.4 %collective-permute-start.4 = (bf16[1024,2048]{1,0:T(8,128)(2,1)}, bf16[1024,2048]{1,0:T(8,128)(2,1)}, u32[]{:S(2)}, u32[]{:S(2)}) collective-permute-start(bf16[1024,2048]{1,0:T(8,128)(2,1)} %slice.97), channel_id=1, source_target_pairs={{0,1},{1,0},{2,3},{3,2},{4,5},{5,4},{6,7},{7,6}} | collective-permute-start | bytes 12582920 | tf_op jit(solution)/shard_map/ppermute | solution.py:402
  1184.5 1.3 copy-start.3
  1187.0 43.6 %collective-permute-start.12 = (bf16[1024,256]{1,0:T(8,128)(2,1)}, bf16[1024,256]{1,0:T(8,128)(2,1)}, u32[]{:S(2)}, u32[]{:S(2)}) collective-permute-start(bf16[1024,256]{1,0:T(8,128)(2,1)} %get-tuple-element.62.refs_5_), channel_id=1, source_target_pairs={{0,1},{1,0},{2,3},{3,2},{4,5},{5,4},{6,7},{7,6}} | collective-permute-start | bytes 1572872 | tf_op jit(solution)/shard_map/ppermute | solution.py:402
  1249.6 75.7 %collective-permute-start.17 = (bf16[4096,256]{1,0:T(8,128)(2,1)}, bf16[4096,256]{1,0:T(8,128)(2,1)}, u32[]{:S(2)}, u32[]{:S(2)}) collective-permute-start(bf16[4096,256]{1,0:T(8,128)(2,1)} %wgrad.5), channel_id=1, source_target_pairs={{0,1},{1,0},{2,3},{3,2},{4,5},{5,4},{6,7},{7,6}} | collective-permute-start | bytes 6291464 | tf_op jit(solution)/shard_map/ppermute | solution.py:402
  1277.1 43.1 %collective-permute-start.13 = (f32[4096]{0:T(1024)}, f32[4096]{0:T(1024)}, u32[]{:S(2)}, u32[]{:S(2)}) collective-permute-start(f32[4096]{0:T(1024)} %bitcast.95), channel_id=1, source_target_pairs={{0,1},{1,0},{2,3},{3,2},{4,5},{5,4},{6,7},{7,6}} | collective-permute-start | bytes 49160 | tf_op jit(solution)/shard_map/ppermute | solution.py:402
  1320.9 3.7 collective-permute-start.14

commit v3 on v2

--- a/solution.py
+++ b/solution.py
@@ -395,8 +395,8 @@
     chips_perm = [(0, 2), (1, 3), (2, 0), (3, 1)]
     cores_perm = [(0, 1), (1, 0), (2, 3), (3, 2)]
 
-    def to_chip(val):
-        return lax.ppermute(val, "sp", chips_perm)
+    def to_chip(val, perm=tuple(chips_perm)):
+        return lax.ppermute(val, "sp", perm)
 
     def to_core(val):
         return lax.ppermute(val, "sp", cores_perm)
@@ -452,8 +452,7 @@
         n_all = [n_own, n_1, n_2, n_3]
         g_all = [out_grad, g_1, g_2, g_3]
 
-        o_all, dq_all = [], []
-        kv_sums = ()
+        o_all = []
         for pair in (0, 1):
             a, b = 2 * pair, 2 * pair + 1
             first_p, token_p = pair_rows(first_key, pair), pair_rows(token, pair)
@@ -461,25 +460,35 @@
             tables = (jnp.concatenate([cos_p, cos_p], axis=1), jnp.concatenate([-sin_p, sin_p], axis=1))
             q = proj_pair(n_all[a], n_all[b], w_q, core_arr, False, tables)
             o, lse = attn_fwd(q, k_all, vt_all, first_p, token_p)
+            o_all.append(o)
+            if pair:
+                continue
             d_o = proj_pair(g_all[a], g_all[b], w_o, core_arr, True)
-            dq, *kv_sums = attn_bwd(q, d_o, o, lse, k_all, kt_all, v_all, first_p, token_p, cos_p, sin_p, kv_sums)
-            o_all.append(o)
-            dq_all.append(dq)
+            dq_own, dk, dv = attn_bwd(q, d_o, o, lse, k_all, kt_all, v_all, first_p, token_p, cos_p, sin_p, ())
 
         block_out = join_heads(o_all[0], to_core(o_all[0][chunk:]), w_o, core_arr, False, (x, b_o[None]))
-        d_normed_q = join_heads(dq_all[0], to_core(dq_all[0][chunk:]), w_q, core_arr, True)
-
-        dk, dv = kv_sums
+        dq_theirs = to_core(dq_own[chunk:])
+        d_normed_q = join_heads(dq_own, dq_theirs, w_q, core_arr, True)
+
+        pair_len = 2 * chunk
+        chip = me // 2
+
+        def chip_rows(val, which):
+            return lax.dynamic_slice_in_dim(val, which * pair_len, pair_len, axis=0)
+
         theirs = to_core(jnp.where(core == 0, dv, dk))
-        mine = jnp.where(core == 0, dk, dv) + theirs
-        turned = rotary(mine[:, None].astype(jnp.bfloat16).astype(jnp.float32), cos_all, -sin_all)[:, 0]
+        part = jnp.where(core == 0, dk, dv) + theirs
+        dq_other = to_chip(dq_own)
+        mine = chip_rows(part, chip) + to_chip(chip_rows(part, 1 - chip), ((2, 0), (3, 1)))
+        turned = rotary(mine[:, None].astype(jnp.bfloat16).astype(jnp.float32), chip_rows(cos_all, chip), -chip_rows(sin_all, chip))[:, 0]
         mine_lin = jnp.where(core == 0, turned, mine).astype(jnp.bfloat16)
-        mine_pieces = [piece_rows(mine_lin, piece) for piece in pieces]
+        other_lin = to_chip(mine_lin)
+        mine_pieces = [lax.dynamic_slice_in_dim(val, which * chunk, chunk, axis=0) for val in (mine_lin, other_lin) for which in (core, 1 - core)]
 
         halves = [(0, 0), (0, 1), (1, 0), (1, 1)]
         w_o_part, w_o_grad, b_o_sum = wgrad([(o_all[i], r) for i, r in halves], [(g, 0) for g in g_all], core_arr, chunk, 512, 1024, 0, True)
         w_o_theirs = to_core(w_o_part)
-        w_q_part, w_q_grad, w_o_grad = wgrad([(n, 0) for n in n_all], [(dq_all[i], r) for i, r in halves], core_arr, chunk, 512, 1024, 1,
+        w_q_part, w_q_grad, w_o_grad = wgrad([(n, 0) for n in n_all], [((dq_own, dq_other)[i], r) for i, r in halves], core_arr, chunk, 512, 1024, 1,
                                              carried=(w_o_theirs, w_o_grad))
         w_q_theirs = to_core(w_q_part)
         mine_w, = wgrad([(n, 0) for n in n_all], [(val, 0) for val in mine_pieces], core_arr, chunk, 1024, HEAD_DIM)
@@ -487,7 +496,8 @@
         w_k_grad = jnp.where(core == 0, mine_w, theirs_w)
         w_v_grad = jnp.where(core == 0, theirs_w, mine_w)
 
-        dkv_tok = ordered(mine_pieces[0], to_core(mine_pieces[1]), 1)
+        lin_theirs = to_core(mine_pieces[1])
+        dkv_tok = ordered(mine_pieces[0], lin_theirs, 1)
         x_grad, gain_part = finish(d_normed_q, x, out_grad, norm_scale, dkv_tok, w_kv)
         w_q_grad = place(w_q_theirs, w_q_grad, core_arr, 1)
         gain_sum = gain_part[0] + to_core(gain_part[0])

time: 1350 us -> 1440 us (1.067)
  waiting for transfers between devices: 352 us -> 555 us
  Pallas kernels: 851 us -> 672 us
  starting transfers between devices: 6.9 us -> 54.5 us
    ppermute x4 -> x7, waiting for transfers between devices: 351 us -> 555 us  [to_chip(): return lax.ppermute(val, 'sp', perm)]
    pallas_call x2 -> x1, Pallas kernels: 222 us -> 86.3 us  [attn_bwd(): pl.pallas_call(functools.partial(bwd_kernel, bq, bk, heads, bool(sums)),...]
    ppermute x4 -> x7, starting transfers between devices: 4.05 us -> 52.2 us  [to_chip(): return lax.ppermute(val, 'sp', perm)]
    pallas_call x4 -> x3, Pallas kernels: 177 us -> 134 us  [proj_pair(): pl.pallas_call(functools.partial(proj_kernel, NT if by_rows else NN, bool...]
    sin x1, other arithmetic: 3.68 us -> 19.2 us  [rope_tables(): return (jnp.cos(angles), jnp.sin(angles))]
  transfers between devices with their start and end apart: 18 -> 21, of which waited for: 3 -> 4; matrix products, arithmetic and copies ran while one was open for 8% -> 8% of each run, Pallas kernels for 56% -> 40%
where the time goes in v3:
time: 1440 us; the launch traced here: 1430 us
  Pallas kernels  672 us (47%)
  waiting for transfers between devices  555 us (39%)
  other arithmetic  73.8 us (5%)
  starting transfers between devices  54.5 us (4%)
  local copies, waits for them, and re-layouts  50.8 us (4%)
    ppermute x7, waiting for transfers between devices, to_chip(): return lax.ppermute(val, 'sp', perm)  555 us
    pallas_call x3, Pallas kernels, wgrad(): pl.pallas_call(functools.partial(wgrad_kernel, len(a), whole_axis is not...  203 us
    pallas_call x3, Pallas kernels, proj_pair(): pl.pallas_call(functools.partial(proj_kernel, NT if by_rows else NN, bool...  134 us
    pallas_call x2, Pallas kernels, attn_fwd(): pl.pallas_call(functools.partial(fwd_kernel, bq, bk, heads), grid_spec=pl...  126 us
    pallas_call x1, Pallas kernels, attn_bwd(): pl.pallas_call(functools.partial(bwd_kernel, bq, bk, heads, bool(sums)),...  86.3 us
    pallas_call x2, Pallas kernels, join_heads(): pl.pallas_call(functools.partial(join_kernel, NT if by_rows else NN, bool...  85.5 us
    ppermute x7, starting transfers between devices, to_chip(): return lax.ppermute(val, 'sp', perm)  52.2 us
  transfers between devices with their start and end apart: 21, of which 4 were waited for; matrix products, arithmetic and copies ran while one was open for 8% of the time, Pallas kernels for 40%

profile of v3, /device:TPU:0, one launch (start us, length us, event | category | flops | bytes accessed | tf_op | source)
XLA Modules:
  0.0 1425.9 jit_solution(13299958118497602659)
XLA Ops:
  0.6 0.7 pad_add_fusion
  1.4 10.0 all_gather.3
  11.3 5.1 fusion
  16.5 10.5 fusion.2.a0_ref.refs_0_
  27.0 2.0 collective-permute-start.15
  29.0 19.2 %multiply_sine_fusion = (f32[4096,64]{1,0:T(8,128)S(1)}, f32[4096,64]{1,0:T(8,128)S(1)}) fusion(f32[64]{0:T(128)S(1)} %negate_power_fusion, f32[4096]{0:T(1024)S(1)} %bitcast.92), kind=kLoop, calls=%fused_computation.6 | loop fusion | flops 262144 | bytes 2113792 | tf_op jit(solution)/shard_map/sin | solution.py:41
  48.3 1.6 constant_dynamic-slice_fusion.3
  50.8 0.9 copy.35
  51.7 1.9 constant_dynamic-update-slice_fusion.1
  54.1 8.5 fusion.24
  63.0 2.5 broadcast_in_dim.40
  65.5 1.6 pad_maximum_fusion.1
  71.2 1.3 maximum_maximum_fusion.rest_0_
  72.5 1.0 maximum_bitcast_fusion.1
  74.0 1.1 fusion.7
  75.1 1.3 maximum_maximum_fusion.1.rest_1_
  77.1 335.3 %collective-permute-done.2 = bf16[1024,512]{0,1:T(8,128)(2,1)} collective-permute-done((bf16[1024,512]{0,1:T(8,128)(2,1)}, bf16[1024,512]{0,1:T(8,128)(2,1)}, u32[]{:S(2)}, u32[]{:S(2)}) %collective-permute-start.2) | collective-permute-done | bytes 1048608 | tf_op jit(solution)/shard_map/ppermute | solution.py:399
  413.0 1.4 maximum_maximum_fusion.3.rest_1_
  415.5 1.1 copy.38.sin_ref
  416.6 1.1 copy.37.cos_ref
  418.3 2.9 maximum_maximum_fusion.2.rest_0_
  421.2 2.3 constant_dynamic-update-slice_fusion.4
  423.5 2.3 constant_dynamic-update-slice_fusion.3
  425.7 2.3 constant_dynamic-update-slice_fusion.2
  428.0 5.4 fusion.22
  433.4 4.1 copy.36.k_ref
  437.5 2.5 copy.40.v_ref
  440.5 44.5 %proj_pair.3.q_ref = bf16[2048,2048]{1,0:T(8,128)(2,1)} custom-call(s32[1]{0:T(128)} %bitcast.core_ref, bf16[1024,4096]{1,0:T(8,128)(2,1)} %fusion.2.a0_ref.refs_0_, bf16[1024,4096]{1,0:T(8,128)(2,1)} %collective-permute-done.a1_ref.refs_1_, bf16[4096,4096]{1,0:T(8,128)(2,1)} %w_ref.5, f32[2048,128]{1,0:T(8,128)} %maximum_maximum_fusion.rest_0_, ...), custom_call_target="tpu_custom_call" | custom-call | flops 34359738368 | bytes 41943040 | tf_op jit(solution)/shard_map/proj_pair/pallas_call | solution.py:85
  485.0 49.7 %attn_fwd.2 = (bf16[2048,2048]{1,0:T(8,128)(2,1)}, f32[8,8,256]{2,1,0:T(8,128)}) custom-call(s32[8]{0:T(128)} %and_select_fusion.5.lo_ref, s32[8]{0:T(128)} %fusion.21.hi_ref, s32[8]{0:T(128)} %copy-done.18, bf16[2048,2048]{1,0:T(8,128)(2,1)} %proj_pair.3.q_ref, bf16[4096,256]{1,0:T(8,128)(2,1)} %copy.36.k_ref, bf16[256,4096]{1,0:T(8,128)(2,1)} %get-tuple-element.50.vt_ref, ...), custom_call_target="tpu_custom_call" | custom-call | flops 34359738368 | bytes 16777216 | tf_op jit(solution)/shard_map/attn_fwd/pallas_call | solution.py:302
  534.7 44.8 %proj_pair.5.q_ref = bf16[2048,2048]{1,0:T(8,128)(2,1)} custom-call(s32[1]{0:T(128)} %bitcast.core_ref, bf16[1024,4096]{1,0:T(8,128)(2,1)} %collective-permute-done.12.a0_ref.refs_2_, bf16[1024,4096]{1,0:T(8,128)(2,1)} %collective-permute-done.13.a1_ref.refs_3_, bf16[4096,4096]{1,0:T(8,128)(2,1)} %w_ref.5, f32[2048,128]{1,0:T(8,128)} %maximum_maximum_fusion.2.rest_0_, ...), custom_call_target="tpu_custom_call" | custom-call | flops 34359738368 | bytes 41943040 | tf_op jit(solution)/shard_map/proj_pair/pallas_call | solution.py:85
  579.5 76.5 %attn_fwd.3 = (bf16[2048,2048]{1,0:T(8,128)(2,1)}, f32[8,8,256]{2,1,0:T(8,128)}) custom-call(s32[8]{0:T(128)} %and_select_fusion.1.lo_ref, s32[8]{0:T(128)} %fusion.19.hi_ref, s32[8]{0:T(128)} %copy-done.19, bf16[2048,2048]{1,0:T(8,128)(2,1)} %proj_pair.5.q_ref, bf16[4096,256]{1,0:T(8,128)(2,1)} %copy.36.k_ref, bf16[256,4096]{1,0:T(8,128)(2,1)} %get-tuple-element.50.vt_ref, ...), custom_call_target="tpu_custom_call" | custom-call | flops 34359738368 | bytes 16777216 | tf_op jit(solution)/shard_map/attn_fwd/pallas_call | solution.py:302
  656.0 87.7 %wgrad.3 = (bf16[2048,4096]{1,0:T(8,128)(2,1)}, bf16[4096,4096]{1,0:T(8,128)(2,1)}, f32[1,4096]{1,0:T(1,128)}) custom-call(s32[1]{0:T(128)} %bitcast.core_ref, bf16[2048,2048]{1,0:T(8,128)(2,1)} %get-tuple-element.27.mine_ref.o_ref.refs_0_.refs_1_, bf16[2048,2048]{1,0:T(8,128)(2,1)} %get-tuple-element.27.mine_ref.o_ref.refs_0_.refs_1_, ...), custom_call_target="tpu_custom_call" | custom-call | flops 68719476736 | bytes 67108864 | tf_op jit(solution)/shard_map/wgrad/pallas_call | solution.py:135
  743.8 44.3 %proj_pair.4.do_ref = bf16[2048,2048]{1,0:T(8,128)(2,1)} custom-call(s32[1]{0:T(128)} %bitcast.core_ref, bf16[1024,4096]{1,0:T(8,128)(2,1)} %bitcast.86, bf16[1024,4096]{1,0:T(8,128)(2,1)} %collective-permute-done.5.a1_ref.refs_5_, bf16[4096,4096]{1,0:T(8,128)(2,1)} %w_ref.4), custom_call_target="tpu_custom_call" | custom-call | flops 34359738368 | bytes 41943040 | tf_op jit(solution)/shard_map/proj_pair/pallas_call | solution.py:85
  788.1 86.3 %attn_bwd.1 = (bf16[2048,2048]{1,0:T(8,128)(2,1)}, f32[4096,256]{1,0:T(8,128)}, f32[4096,256]{1,0:T(8,128)}) custom-call(s32[4]{0:T(128)} %and_select_fusion.3.lo_ref, s32[4]{0:T(128)} %fusion.20.hi_ref, s32[4]{0:T(128)} %copy-done.17, bf16[2048,2048]{1,0:T(8,128)(2,1)} %proj_pair.3.q_ref, bf16[2048,2048]{1,0:T(8,128)(2,1)} %proj_pair.4.do_ref, ...), custom_call_target="tpu_custom_call" | custom-call | flops 85899345920 | bytes 33554432 | tf_op jit(solution)/shard_map/attn_bwd/pallas_call | solution.py:374
  874.4 46.6 %collective-permute-start.14 = (bf16[2048,2048]{1,0:T(8,128)(2,1)}, bf16[2048,2048]{1,0:T(8,128)(2,1)}, u32[]{:S(2)}, u32[]{:S(2)}) collective-permute-start(bf16[2048,2048]{1,0:T(8,128)(2,1)} %get-tuple-element.30.mine_ref.refs_4_.refs_5_), channel_id=1, source_target_pairs={{0,2},{1,3},{2,0},{3,1},{4,6},{5,7},{6,4},{7,5}} | collective-permute-start | bytes 25165832 | tf_op jit(solution)/shard_map/ppermute | solution.py:399
  921.0 4.7 broadcast_select_fusion.2
  925.9 176.5 %collective-permute-done.14.refs_6_.refs_7_ = bf16[2048,2048]{1,0:T(8,128)(2,1)} collective-permute-done((bf16[2048,2048]{1,0:T(8,128)(2,1)}, bf16[2048,2048]{1,0:T(8,128)(2,1)}, u32[]{:S(2)}, u32[]{:S(2)}) %collective-permute-start.14) | collective-permute-done | bytes 8388640 | tf_op jit(solution)/shard_map/ppermute | solution.py:399
  1102.4 98.2 %wgrad.4 = (bf16[4096,2048]{1,0:T(8,128)(2,1)}, bf16[4096,4096]{1,0:T(8,128)(2,1)}, bf16[4096,4096]{1,0:T(8,128)(2,1)}) custom-call(s32[1]{0:T(128)} %bitcast.core_ref, bf16[1024,4096]{1,0:T(8,128)(2,1)} %fusion.2.a0_ref.refs_0_, bf16[1024,4096]{1,0:T(8,128)(2,1)} %collective-permute-done.a1_ref.refs_1_, ...), custom_call_target="tpu_custom_call", output_to_operand_aliasing={{2}: (10, {})} | custom-call | flops 68719476736 | bytes 67108864 | tf_op jit(solution)/shard_map/wgrad/pallas_call | solution.py:135
  1200.7 5.1 slice.94
  1206.9 3.0 select_add_fusion
  1209.9 2.1 copy-done
  1212.0 1.5 constant_dynamic-slice_fusion.8
  1213.4 1.3 collective-permute-start.8
  1215.4 4.9 slice.91
  1220.7 42.8 %collective-permute-done.8 = f32[2048,256]{1,0:T(8,128)S(1)} collective-permute-done((f32[2048,256]{1,0:T(8,128)}, f32[2048,256]{1,0:T(8,128)S(1)}, u32[]{:S(2)}, u32[]{:S(2)}) %collective-permute-start.8) | collective-permute-done | bytes 2097184 | tf_op jit(solution)/shard_map/ppermute | solution.py:399
  1264.4 0.8 fusion.4
  1265.2 1.0 copy-done.12
  1266.2 0.8 constant_dynamic-slice_fusion.6.refs_5_
  1267.0 42.7 %join_heads.3.y_ref = f32[1024,4096]{1,0:T(8,128)} custom-call(s32[1]{0:T(128)} %bitcast.core_ref, bf16[2048,2048]{1,0:T(8,128)(2,1)} %get-tuple-element.30.mine_ref.refs_4_.refs_5_, bf16[1024,2048]{1,0:T(8,128)(2,1)} %collective-permute-done.6.theirs_ref, bf16[4096,4096]{1,0:T(8,128)(2,1)} %w_ref.5, bf16[4096,4096]{1,0:T(8,128)(2,1)} %w_ref.5), custom_call_target="tpu_custom_call" | custom-call | flops 34359738368 | bytes 58720256 | tf_op jit(solution)/shard_map/join_heads/pallas_call | solution.py:193
  1309.7 1.2 broadcast_select_fusion.4
  1311.0 0.8 copy-done.9
  1311.7 1.1 broadcast_select_fusion.3
  1312.8 1.1 pad_maximum_fusion.2.dkv_ref
  1313.9 23.8 %finish.1 = (bf16[1024,4096]{1,0:T(8,128)(2,1)}, f32[1,4096]{1,0:T(1,128)}) custom-call(f32[1024,4096]{1,0:T(8,128)} %join_heads.3.y_ref, bf16[1024,4096]{1,0:T(8,128)(2,1)} %bitcast.81, bf16[1024,4096]{1,0:T(8,128)(2,1)} %bitcast.87, bf16[1,4096]{1,0:T(2,128)(2,1)} %broadcast_in_dim.46.gain_ref, bf16[1024,512]{1,0:T(8,128)(2,1)} %pad_maximum_fusion.2.dkv_ref, ...), custom_call_target="tpu_custom_call" | custom-call | flops 4294967296 | bytes 41943040 | tf_op jit(solution)/shard_map/finish/pallas_call | solution.py:225
  1337.7 1.3 broadcast_in_dim.44.rest_1_
  1339.1 1.3 add.134
  1340.4 2.0 collective-permute-start.11
  1342.4 2.2 constant_dynamic-slice_fusion
  1344.7 16.8 %wgrad.5 = bf16[4096,256]{1,0:T(8,128)(2,1)} custom-call(s32[1]{0:T(128)} %bitcast.core_ref, bf16[1024,4096]{1,0:T(8,128)(2,1)} %fusion.2.a0_ref.refs_0_, bf16[1024,4096]{1,0:T(8,128)(2,1)} %collective-permute-done.a1_ref.refs_1_, bf16[1024,4096]{1,0:T(8,128)(2,1)} %collective-permute-done.12.a0_ref.refs_2_, ...), custom_call_target="tpu_custom_call" | custom-call | flops 8589934592 | bytes 37748736 | tf_op jit(solution)/shard_map/wgrad/pallas_call | solution.py:135
  1361.6 42.8 %join_heads.2 = bf16[1024,4096]{1,0:T(8,128)(2,1)} custom-call(s32[1]{0:T(128)} %bitcast.core_ref, bf16[2048,2048]{1,0:T(8,128)(2,1)} %get-tuple-element.27.mine_ref.o_ref.refs_0_.refs_1_, bf16[1024,2048]{1,0:T(8,128)(2,1)} %collective-permute-done.4.theirs_ref, bf16[4096,4096]{1,0:T(8,128)(2,1)} %w_ref.4, bf16[4096,4096]{1,0:T(8,128)(2,1)} %w_ref.4, ...), custom_call_target="tpu_custom_call" | custom-call | flops 34359738368 | bytes 58720256 | tf_op jit(solution)/shard_map/join_heads/pallas_call | solution.py:193
  1404.4 1.3 add_convert_fusion
  1405.7 1.4 convert_reduce_fusion
  1407.1 4.5 broadcast_select_fusion
  1411.6 13.8 place.1
  (124 shorter events, 13.3 us)
Async XLA Ops:
  11.3 5.1 copy-start.15
  27.0 413.5 %collective-permute-start = (bf16[1024,4096]{1,0:T(8,128)(2,1)}, bf16[1024,4096]{1,0:T(8,128)(2,1)}, u32[]{:S(2)}, u32[]{:S(2)}) collective-permute-start(bf16[1024,4096]{1,0:T(8,128)(2,1)} %fusion.2.a0_ref.refs_0_), channel_id=1, source_target_pairs={{0,1},{1,0},{2,3},{3,2},{4,5},{5,4},{6,7},{7,6}} | collective-permute-start | bytes 25165832 | tf_op jit(solution)/shard_map/ppermute | solution.py:402
  27.0 387.4 %collective-permute-start.12 = (bf16[1024,4096]{1,0:T(8,128)(2,1)}, bf16[1024,4096]{1,0:T(8,128)(2,1)}, u32[]{:S(2)}, u32[]{:S(2)}) collective-permute-start(bf16[1024,4096]{1,0:T(8,128)(2,1)} %fusion.2.a0_ref.refs_0_), channel_id=1, source_target_pairs={{0,2},{1,3},{2,0},{3,1},{4,6},{5,7},{6,4},{7,5}} | collective-permute-start | bytes 25165832 | tf_op jit(solution)/shard_map/ppermute | solution.py:399
  27.0 413.0 %collective-permute-start.15 = (bf16[1024,4096]{1,0:T(8,128)(2,1)}, bf16[1024,4096]{1,0:T(8,128)(2,1)}, u32[]{:S(2)}, u32[]{:S(2)}) collective-permute-start(bf16[1024,4096]{1,0:T(8,128)(2,1)} %bitcast.83), channel_id=1, source_target_pairs={{0,2},{1,3},{2,0},{3,1},{4,6},{5,7},{6,4},{7,5}} | collective-permute-start | bytes 25165832 | tf_op jit(solution)/shard_map/ppermute | solution.py:399
  48.3 1.7 copy-start.4
  48.3 2.3 copy-start.6
  51.7 2.2 copy-start.13
  54.0 8.6 copy-start.8
  54.1 8.8 copy-start.14
  67.1 354.1 %collective-permute-start.1 = (bf16[1024,512]{0,1:T(8,128)(2,1)}, bf16[1024,512]{0,1:T(8,128)(2,1)}, u32[]{:S(2)}, u32[]{:S(2)}) collective-permute-start(bf16[1024,512]{0,1:T(8,128)(2,1)} %get-tuple-element.66), channel_id=1, source_target_pairs={{0,1},{1,0},{2,3},{3,2},{4,5},{5,4},{6,7},{7,6}} | collective-permute-start | bytes 3145736 | tf_op jit(solution)/shard_map/ppermute | solution.py:402
  67.1 345.3 %collective-permute-start.2 = (bf16[1024,512]{0,1:T(8,128)(2,1)}, bf16[1024,512]{0,1:T(8,128)(2,1)}, u32[]{:S(2)}, u32[]{:S(2)}) collective-permute-start(bf16[1024,512]{0,1:T(8,128)(2,1)} %get-tuple-element.66), channel_id=1, source_target_pairs={{0,2},{1,3},{2,0},{3,1},{4,6},{5,7},{6,4},{7,5}} | collective-permute-start | bytes 3145736 | tf_op jit(solution)/shard_map/ppermute | solution.py:399
  68.5 0.9 copy-start.18
  68.7 7.8 copy-start.17
  68.8 7.7 copy-start.19
  76.5 339.0 %copy-start.10 = (f32[64,2048]{0,1:T(8,128)S(1)}, f32[64,2048]{0,1:T(8,128)}, u32[]{:S(2)}) copy-start(f32[64,2048]{0,1:T(8,128)} %get-tuple-element.64) | copy-start | bytes 1572868
  76.5 340.2 %copy-start.11 = (f32[64,2048]{0,1:T(8,128)S(1)}, f32[64,2048]{0,1:T(8,128)}, u32[]{:S(2)}) copy-start(f32[64,2048]{0,1:T(8,128)} %maximum_bitcast_fusion.1) | copy-start | bytes 1572868
  412.4 13.4 collective-permute-start.3
  414.4 120.3 %collective-permute-start.13 = (bf16[1024,4096]{1,0:T(8,128)(2,1)}, bf16[1024,4096]{1,0:T(8,128)(2,1)}, u32[]{:S(2)}, u32[]{:S(2)}) collective-permute-start(bf16[1024,4096]{1,0:T(8,128)(2,1)} %collective-permute-done.12.a0_ref.refs_2_), channel_id=1, source_target_pairs={{0,1},{1,0},{2,3},{3,2},{4,5},{5,4},{6,7},{7,6}} | collective-permute-start | bytes 25165832 | tf_op jit(solution)/shard_map/ppermute | solution.py:402
  421.2 234.8 %collective-permute-start.5 = (bf16[1024,4096]{1,0:T(8,128)(2,1)}, bf16[1024,4096]{1,0:T(8,128)(2,1)}, u32[]{:S(2)}, u32[]{:S(2)}) collective-permute-start(bf16[1024,4096]{1,0:T(8,128)(2,1)} %bitcast.84), channel_id=1, source_target_pairs={{0,1},{1,0},{2,3},{3,2},{4,5},{5,4},{6,7},{7,6}} | collective-permute-start | bytes 25165832 | tf_op jit(solution)/shard_map/ppermute | solution.py:402
  440.0 216.0 %collective-permute-start.16 = (bf16[1024,4096]{1,0:T(8,128)(2,1)}, bf16[1024,4096]{1,0:T(8,128)(2,1)}, u32[]{:S(2)}, u32[]{:S(2)}) collective-permute-start(bf16[1024,4096]{1,0:T(8,128)(2,1)} %collective-permute-done.15.refs_6_), channel_id=1, source_target_pairs={{0,1},{1,0},{2,3},{3,2},{4,5},{5,4},{6,7},{7,6}} | collective-permute-start | bytes 25165832 | tf_op jit(solution)/shard_map/ppermute | solution.py:402
  743.8 358.7 %collective-permute-start.17 = (bf16[2048,4096]{1,0:T(8,128)(2,1)}, bf16[2048,4096]{1,0:T(8,128)(2,1)}, u32[]{:S(2)}, u32[]{:S(2)}) collective-permute-start(bf16[2048,4096]{1,0:T(8,128)(2,1)} %get-tuple-element.36), channel_id=1, source_target_pairs={{0,1},{1,0},{2,3},{3,2},{4,5},{5,4},{6,7},{7,6}} | collective-permute-start | bytes 50331656 | tf_op jit(solution)/shard_map/ppermute | solution.py:402
  874.4 228.0 %collective-permute-start.14 = (bf16[2048,2048]{1,0:T(8,128)(2,1)}, bf16[2048,2048]{1,0:T(8,128)(2,1)}, u32[]{:S(2)}, u32[]{:S(2)}) collective-permute-start(bf16[2048,2048]{1,0:T(8,128)(2,1)} %get-tuple-element.30.mine_ref.refs_4_.refs_5_), channel_id=1, source_target_pairs={{0,2},{1,3},{2,0},{3,1},{4,6},{5,7},{6,4},{7,5}} | collective-permute-start | bytes 25165832 | tf_op jit(solution)/shard_map/ppermute | solution.py:399
  925.7 280.5 %collective-permute-start.7 = (f32[4096,256]{1,0:T(8,128)}, f32[4096,256]{1,0:T(8,128)}, u32[]{:S(2)}, u32[]{:S(2)}) collective-permute-start(f32[4096,256]{1,0:T(8,128)} %broadcast_select_fusion.2), channel_id=1, source_target_pairs={{0,1},{1,0},{2,3},{3,2},{4,5},{5,4},{6,7},{7,6}} | collective-permute-start | bytes 12582920 | tf_op jit(solution)/shard_map/ppermute | solution.py:402
  1200.6 211.0 %collective-permute-start.18 = (bf16[4096,2048]{1,0:T(8,128)(2,1)}, bf16[4096,2048]{1,0:T(8,128)(2,1)}, u32[]{:S(2)}, u32[]{:S(2)}) collective-permute-start(bf16[4096,2048]{1,0:T(8,128)(2,1)} %get-tuple-element.38), channel_id=1, source_target_pairs={{0,1},{1,0},{2,3},{3,2},{4,5},{5,4},{6,7},{7,6}} | collective-permute-start | bytes 50331656 | tf_op jit(solution)/shard_map/ppermute | solution.py:402
  1200.6 5.5 copy-start.2
  1200.7 6.2 copy-start.3
  1205.7 61.3 %collective-permute-start.6 = (bf16[1024,2048]{1,0:T(8,128)(2,1)}, bf16[1024,2048]{1,0:T(8,128)(2,1)}, u32[]{:S(2)}, u32[]{:S(2)}) collective-permute-start(bf16[1024,2048]{1,0:T(8,128)(2,1)} %slice.94), channel_id=1, source_target_pairs={{0,1},{1,0},{2,3},{3,2},{4,5},{5,4},{6,7},{7,6}} | collective-permute-start | bytes 12582920 | tf_op jit(solution)/shard_map/ppermute | solution.py:402
  1209.9 2.1 copy-start
  1212.0 2.8 copy-start.16
  1213.4 50.1 %collective-permute-start.8 = (f32[2048,256]{1,0:T(8,128)}, f32[2048,256]{1,0:T(8,128)S(1)}, u32[]{:S(2)}, u32[]{:S(2)}) collective-permute-start(f32[2048,256]{1,0:T(8,128)} %constant_dynamic-slice_fusion.8), channel_id=1, source_target_pairs={{2,0},{3,1},{6,4},{7,5}} | collective-permute-start | bytes 6291464 | tf_op jit(solution)/shard_map/ppermute | solution.py:399
  1215.4 48.2 %copy-start.1 = (f32[4096,256]{1,0:T(8,128)S(1)}, f32[4096,256]{1,0:T(8,128)}, u32[]{:S(2)}) copy-start(f32[4096,256]{1,0:T(8,128)} %copy-done) | copy-start | bytes 12582916
  1220.3 43.6 %copy-start.5 = (f32[4096,64]{1,0:T(8,128)S(1)}, f32[4096,64]{1,0:T(8,128)}, u32[]{:S(2)}) copy-start(f32[4096,64]{1,0:T(8,128)} %copy-done.4) | copy-start | bytes 3145732
  1220.3 43.6 %copy-start.7 = (f32[4096,64]{1,0:T(8,128)S(1)}, f32[4096,64]{1,0:T(8,128)}, u32[]{:S(2)}) copy-start(f32[4096,64]{1,0:T(8,128)} %copy-done.6) | copy-start | bytes 3145732
  1220.3 141.3 %collective-permute-start.4 = (bf16[1024,2048]{1,0:T(8,128)(2,1)}, bf16[1024,2048]{1,0:T(8,128)(2,1)}, u32[]{:S(2)}, u32[]{:S(2)}) collective-permute-start(bf16[1024,2048]{1,0:T(8,128)(2,1)} %slice.91), channel_id=1, source_target_pairs={{0,1},{1,0},{2,3},{3,2},{4,5},{5,4},{6,7},{7,6}} | collective-permute-start | bytes 12582920 | tf_op jit(solution)/shard_map/ppermute | solution.py:402
  1265.2 1.0 copy-start.12
  1267.0 42.7 %collective-permute-start.9 = (bf16[1024,256]{1,0:T(8,128)(2,1)}, bf16[1024,256]{1,0:T(8,128)(2,1)}, u32[]{:S(2)}, u32[]{:S(2)}) collective-permute-start(bf16[1024,256]{1,0:T(8,128)(2,1)} %constant_dynamic-slice_fusion.6.refs_5_), channel_id=1, source_target_pairs={{0,1},{1,0},{2,3},{3,2},{4,5},{5,4},{6,7},{7,6}} | collective-permute-start | bytes 1572872 | tf_op jit(solution)/shard_map/ppermute | solution.py:402
  1309.7 32.7 %collective-permute-start.19 = (bf16[2048,256]{1,0:T(8,128)(2,1)}, bf16[2048,256]{1,0:T(8,128)(2,1)}, u32[]{:S(2)}, u32[]{:S(2)}) collective-permute-start(bf16[2048,256]{1,0:T(8,128)(2,1)} %copy-done.12), channel_id=1, source_target_pairs={{0,2},{1,3},{2,0},{3,1},{4,6},{5,7},{6,4},{7,5}} | collective-permute-start | bytes 3145736 | tf_op jit(solution)/shard_map/ppermute | solution.py:399
  1311.0 0.8 copy-start.9
  1337.7 1.4 collective-permute-start.10
  1340.4 64.0 %collective-permute-start.11 = (f32[4096]{0:T(1024)}, f32[4096]{0:T(1024)}, u32[]{:S(2)}, u32[]{:S(2)}) collective-permute-start(f32[4096]{0:T(1024)} %add.134), channel_id=1, source_target_pairs={{0,2},{1,3},{2,0},{3,1},{4,6},{5,7},{6,4},{7,5}} | collective-permute-start | bytes 49160 | tf_op jit(solution)/shard_map/ppermute | solution.py:399
  1361.4 45.7 %collective-permute-start.20 = (bf16[4096,256]{1,0:T(8,128)(2,1)}, bf16[4096,256]{1,0:T(8,128)(2,1)}, u32[]{:S(2)}, u32[]{:S(2)}) collective-permute-start(bf16[4096,256]{1,0:T(8,128)(2,1)} %wgrad.5), channel_id=1, source_target_pairs={{0,1},{1,0},{2,3},{3,2},{4,5},{5,4},{6,7},{7,6}} | collective-permute-start | bytes 6291464 | tf_op jit(solution)/shard_map/ppermute | solution.py:402
